TPU v7x, 32 devices: a whole 2x2x4 slice. The times are simulated.
32 devices in a mesh: dp: 4 (over z), row: 4 (over y, x), col: 2 (over core).
Axes of the slice: x: 2, y: 2, z: 4, core: 2. Of those that a mesh axis runs over, the one named last changes fastest.
Arguments:
- block_input: bfloat16 [1536, 2048], P('dp', 'row'), may hold values from -6 to 6
- segments: int32 [4, 384], P('dp'), may hold values from 0 to 5, never falling along the last dimension, each value on 1 to 192 neighbouring positions
- attention_norm: float32 [2048], P('row'), may hold values from 0.5 to 1.5
- query_weight: bfloat16 [2048, 2048], P('row', 'col'), may hold values from -0.125 to 0.125
- key_weight: bfloat16 [2048, 1024], P('row', 'col'), may hold values from -0.125 to 0.125
- value_weight: bfloat16 [2048, 1024], P('row', 'col'), may hold values from -0.125 to 0.125
- query_norm: float32 [128], replicated, may hold values from 0.5 to 1.5
- key_norm: float32 [128], replicated, may hold values from 0.5 to 1.5
- output_weight: bfloat16 [2048, 2048], P('col', 'row'), may hold values from -0.5 to 0.5
- feedforward_norm: float32 [2048], P('row'), may hold values from 0.5 to 1.5
- gate_weight: bfloat16 [2048, 6144], P('row', 'col'), may hold values from -0.125 to 0.125
- up_weight: bfloat16 [2048, 6144], P('row', 'col'), may hold values from -0.125 to 0.125
- down_weight: bfloat16 [6144, 2048], P('col', 'row'), may hold values from -0.15625 to 0.15625
- cotangent: bfloat16 [1536, 2048], P('dp', 'row'), may hold values from -6 to 6
Outputs:
- block_output: bfloat16 [1536, 2048], P('dp', 'row')
- input_gradient: float32 [1536, 2048], P('dp', 'row')
- attention_norm_gradient: float32 [2048], P('row')
- query_gradient: float32 [2048, 2048], P('row', 'col')
- key_gradient: float32 [2048, 1024], P('row', 'col')
- value_gradient: float32 [2048, 1024], P('row', 'col')
- query_norm_gradient: float32 [128], replicated
- key_norm_gradient: float32 [128], replicated
- output_gradient: float32 [2048, 2048], P('col', 'row')
- feedforward_norm_gradient: float32 [2048], P('row')
- gate_gradient: float32 [2048, 6144], P('row', 'col')
- up_gradient: float32 [2048, 6144], P('row', 'col')
- down_gradient: float32 [6144, 2048], P('col', 'row')
Inputs may be any that keep to these rules, and one draw needn't show every extreme that they name: `segments`: along each row sequence numbers never fall; each of the 6 sequences of a batch spans 1 to 192 tokens, and one spans exactly 192.
All inputs are finite; a program needn't handle non-finite values.
Results may differ from a plain program's by a relative error of at most 0.018.
Values may be sent and summed in bfloat16 or wider, within the bound.
A program may use at most 192 MiB of HBM per device.

v0:
```python
from functools import partial

import jax
import jax.numpy as jnp
from jax import lax
from jax.sharding import PartitionSpec as P

epsilon = 1e-06
rope_base = 1000000.0


def rotate_half(values):
    half = values.shape[-1] // 2
    return jnp.concatenate([-values[..., half:], values[..., :half]], axis=-1)


def positions_of(segment_row):
    length = segment_row.shape[0]
    index = jnp.arange(length, dtype=jnp.int32)
    starts = jnp.concatenate([jnp.ones((1,), jnp.bool_), segment_row[1:] != segment_row[:-1]])
    first = lax.cummax(jnp.where(starts, index, jnp.zeros_like(index)), axis=0)
    return index - first


def rotary_tables(positions, head_size):
    half = head_size // 2
    inverse = rope_base ** (-2.0 * jnp.arange(half, dtype=jnp.float32) / head_size)
    angles = positions.astype(jnp.float32)[:, None] * inverse[None, :]
    angles = jnp.concatenate([angles, angles], axis=-1)
    return (jnp.cos(angles)[:, None, :], jnp.sin(angles)[:, None, :])


def head_forward(raw, gain, cosine, sine):
    scale = lax.rsqrt(jnp.mean(raw * raw, axis=-1, keepdims=True) + epsilon)
    normed = raw * scale * gain
    return normed * cosine + rotate_half(normed) * sine


def width_total(values):
    return lax.psum(jnp.sum(values, axis=1, keepdims=True), "row")


def column_total(values):
    return lax.psum(values, "col")


def device_major(matrices, parts):
    return jnp.concatenate(
        [matrix.reshape(matrix.shape[0], parts, -1) for matrix in matrices], axis=2
    ).reshape(matrices[0].shape[0], -1)


def split_major(matrix, widths, parts):
    cube = matrix.reshape(matrix.shape[0], parts, -1)
    pieces = []
    offset = 0
    for member_width in widths:
        piece_width = member_width // parts
        pieces.append(
            cube[:, :, offset : offset + piece_width].reshape(matrix.shape[0], member_width)
        )
        offset = offset + piece_width
    return pieces


def project_in(normed, merged):
    partial_sum = jnp.dot(normed, merged, preferred_element_type=jnp.float32)
    return lax.psum_scatter(partial_sum, "row", scatter_dimension=1, tiled=True)


def project_out(local, weight):
    return jnp.dot(
        lax.all_gather(local, "row", axis=1, tiled=True), weight, preferred_element_type=jnp.float32
    )


def project_back(incoming, weight):
    contract = (((1,), (1,)), ((), ()))
    partial_sum = lax.dot_general(incoming, weight, contract, preferred_element_type=jnp.float32)
    return lax.psum_scatter(partial_sum, "row", scatter_dimension=1, tiled=True)


def weight_gradient(local, incoming):
    return lax.dot_general(
        lax.all_gather(local, "row", axis=1, tiled=True),
        incoming,
        (((0,), (0,)), ((), ())),
        preferred_element_type=jnp.float32,
    )


def input_gradients(local, normed, merged):
    piece = lax.all_gather(local, "row", axis=1, tiled=True)
    block = lax.dot_general(
        normed, piece, (((0,), (0,)), ((), ())), preferred_element_type=jnp.float32
    )
    partial_sum = lax.dot_general(
        piece, merged, (((1,), (1,)), ((), ())), preferred_element_type=jnp.float32
    )
    return (block, partial_sum)


def allowed_pairs(segment_row, key_start, block):
    query_index = jnp.arange(block)
    key_index = jnp.arange(block) + key_start
    return (segment_row[:, None] == segment_row[None, :]) & (
        key_index[None, :] <= query_index[:, None]
    )


def exp_scores(query_block, key_block, allowed, scale):
    scores = (
        jnp.einsum("qhgd,khd->hgqk", query_block, key_block, preferred_element_type=jnp.float32)
        * scale
    )
    return jnp.where(allowed[None, None], jnp.exp(scores), 0.0)


def value_product(shares_low, value_block):
    return jnp.einsum("hgqk,khd->qhgd", shares_low, value_block, preferred_element_type=jnp.float32)


def attention_forward(query_low, key_low, value_low, segment_row, block, scale):
    actives = []
    key_part = 0
    key_start = key_part * block
    allowed = allowed_pairs(segment_row, key_start, block)
    compute = partial(exp_scores, query_low, key_low, allowed, scale)
    numerators = [compute()]
    actives.append(None)
    total = sum((jnp.sum(numerator, axis=-1) for numerator in numerators))
    key_part = 0
    shares_low = (numerators[key_part] / total[..., None]).astype(jnp.bfloat16)
    compute = partial(value_product, shares_low, value_low)
    output = compute()
    outputs = output.astype(jnp.bfloat16)
    return (outputs, total)


def pair_gradients(
    query_block, key_block, value_block, incoming_block, allowed, total_block, delta_block, scale
):
    shares = exp_scores(query_block, key_block, allowed, scale) / total_block[..., None]
    shares_low = shares.astype(jnp.bfloat16)
    value_part = jnp.einsum(
        "hgqk,qhgd->khd", shares_low, incoming_block, preferred_element_type=jnp.float32
    )
    share_back = jnp.einsum(
        "qhgd,khd->hgqk", incoming_block, value_block, preferred_element_type=jnp.float32
    )
    score_back = (shares * (share_back - delta_block[..., None])).astype(jnp.bfloat16)
    query_part = scale * jnp.einsum(
        "hgqk,khd->qhgd", score_back, key_block, preferred_element_type=jnp.float32
    )
    key_part = scale * jnp.einsum(
        "hgqk,qhgd->khd", score_back, query_block, preferred_element_type=jnp.float32
    )
    return (query_part, key_part, value_part)


def attention_backward(
    query_low, key_low, value_low, mixed_low, incoming_low, totals, segment_row, block, scale
):
    tokens, key_heads, group, head_size = query_low.shape
    delta = jnp.transpose(
        jnp.sum(incoming_low.astype(jnp.float32) * mixed_low.astype(jnp.float32), axis=-1),
        (1, 2, 0),
    )
    key_shape = (block, key_heads, head_size)
    key_backs = [jnp.zeros(key_shape, jnp.float32)]
    value_backs = [jnp.zeros(key_shape, jnp.float32)]
    allowed = allowed_pairs(segment_row, 0, block)
    compute = partial(
        pair_gradients, query_low, key_low, value_low, incoming_low, allowed, totals, delta, scale
    )
    pieces = compute()
    accumulated = pieces[0]
    key_backs[0] = pieces[1]
    value_backs[0] = pieces[2]
    return (accumulated, key_backs[0], value_backs[0])


def per_device(
    block_input,
    segments,
    attention_norm,
    query_weight,
    key_weight,
    value_weight,
    query_norm,
    key_norm,
    output_weight,
    feedforward_norm,
    gate_weight,
    up_weight,
    down_weight,
    cotangent,
):
    parts = lax.axis_size("row")
    tokens = block_input.shape[0]
    width = block_input.shape[1] * parts
    head_size = query_norm.shape[0]
    scale = head_size ** (-0.5)
    block = tokens // ((tokens + 511) // 512)
    segment_row = segments[0]
    cosine, sine = rotary_tables(positions_of(segment_row), head_size)
    rotary = partial(head_forward, cosine=cosine, sine=sine)
    residual = block_input.astype(jnp.float32)
    first_scale = lax.rsqrt(width_total(residual * residual) / width + epsilon)
    first_unit = residual * first_scale
    first_normed = (first_unit * attention_norm).astype(jnp.bfloat16)
    attention_widths = (query_weight.shape[1], key_weight.shape[1], value_weight.shape[1])
    attention_merged = device_major((query_weight, key_weight, value_weight), parts)
    projected = project_in(first_normed, attention_merged)
    query_width = attention_widths[0] // parts
    key_width = attention_widths[1] // parts
    key_heads = key_width // head_size
    group = query_width // key_width
    query_raw = projected[:, :query_width].reshape(tokens, key_heads * group, head_size)
    key_raw = projected[:, query_width : query_width + key_width].reshape(
        tokens, key_heads, head_size
    )
    value_raw = projected[:, query_width + key_width :].reshape(tokens, key_heads, head_size)
    query_rot, query_pull = jax.vjp(rotary, query_raw, query_norm)
    key_rot, key_pull = jax.vjp(rotary, key_raw, key_norm)
    query_low = query_rot.astype(jnp.bfloat16).reshape(tokens, key_heads, group, head_size)
    key_low = key_rot.astype(jnp.bfloat16)
    value_low = value_raw.astype(jnp.bfloat16)
    mixed_low, totals = attention_forward(query_low, key_low, value_low, segment_row, block, scale)
    mixed_flat = mixed_low.reshape(tokens, query_width)
    middle = residual + column_total(project_out(mixed_flat, output_weight))
    second_scale = lax.rsqrt(width_total(middle * middle) / width + epsilon)
    second_unit = middle * second_scale
    second_normed = (second_unit * feedforward_norm).astype(jnp.bfloat16)
    feed_widths = (gate_weight.shape[1], up_weight.shape[1])
    feed_merged = device_major((gate_weight, up_weight), parts)
    hidden_width = feed_widths[0] // parts
    gated = project_in(second_normed, feed_merged)
    gate = gated[:, :hidden_width]
    upward = gated[:, hidden_width:]
    gate_sigmoid = jax.nn.sigmoid(gate)
    gate_silu = gate * gate_sigmoid
    hidden = (gate_silu * upward).astype(jnp.bfloat16)
    block_output = (middle + column_total(project_out(hidden, down_weight))).astype(jnp.bfloat16)
    hidden_back = project_back(cotangent, down_weight)
    down_sum = weight_gradient(hidden, cotangent)
    gate_back = (hidden_back * upward * gate_sigmoid * (1.0 + gate * (1.0 - gate_sigmoid))).astype(
        jnp.bfloat16
    )
    up_back = (hidden_back * gate_silu).astype(jnp.bfloat16)
    feed_gradient, second_partial = input_gradients(
        jnp.concatenate([gate_back, up_back], axis=1), second_normed, feed_merged
    )
    gate_sum, up_sum = split_major(feed_gradient, feed_widths, parts)
    second_back = column_total(second_partial)
    feed_sum = jnp.sum(second_back * second_unit, axis=0)
    unit_back = second_back * feedforward_norm
    middle_back = cotangent.astype(jnp.float32) + second_scale * (
        unit_back - second_unit * width_total(unit_back * second_unit) / width
    )
    middle_low = middle_back.astype(jnp.bfloat16)
    mixed_back = project_back(middle_low, output_weight)
    output_sum = weight_gradient(mixed_flat, middle_low)
    incoming_low = mixed_back.astype(jnp.bfloat16).reshape(tokens, key_heads, group, head_size)
    query_back, key_back, value_back = attention_backward(
        query_low, key_low, value_low, mixed_low, incoming_low, totals, segment_row, block, scale
    )
    query_raw_back, query_gain_back = query_pull(
        query_back.reshape(tokens, key_heads * group, head_size)
    )
    key_raw_back, key_gain_back = key_pull(key_back)
    query_low_back = query_raw_back.reshape(tokens, query_width).astype(jnp.bfloat16)
    key_low_back = key_raw_back.reshape(tokens, key_width).astype(jnp.bfloat16)
    value_low_back = value_back.reshape(tokens, key_width).astype(jnp.bfloat16)
    attention_gradient, first_partial = input_gradients(
        jnp.concatenate([query_low_back, key_low_back, value_low_back], axis=1),
        first_normed,
        attention_merged,
    )
    query_sum, key_sum, value_sum = split_major(attention_gradient, attention_widths, parts)
    first_back = column_total(first_partial)
    attention_sum = jnp.sum(first_back * first_unit, axis=0)
    first_unit_back = first_back * attention_norm
    input_gradient = middle_back + first_scale * (
        first_unit_back - first_unit * width_total(first_unit_back * first_unit) / width
    )
    query_gain_sum, key_gain_sum = lax.psum((query_gain_back, key_gain_back), ("dp", "row", "col"))
    summed = (
        lax.psum(attention_sum.astype(jnp.bfloat16), "dp").astype(jnp.float32),
        lax.psum(query_sum.astype(jnp.bfloat16), "dp").astype(jnp.float32),
        lax.psum(key_sum.astype(jnp.bfloat16), "dp").astype(jnp.float32),
        lax.psum(value_sum.astype(jnp.bfloat16), "dp").astype(jnp.float32),
        lax.psum(output_sum.astype(jnp.bfloat16), "dp").astype(jnp.float32),
        lax.psum(feed_sum.astype(jnp.bfloat16), "dp").astype(jnp.float32),
        lax.psum(gate_sum.astype(jnp.bfloat16), "dp").astype(jnp.float32),
        lax.psum(up_sum.astype(jnp.bfloat16), "dp").astype(jnp.float32),
        lax.psum(down_sum.astype(jnp.bfloat16), "dp").astype(jnp.float32),
    )
    return (
        block_output,
        input_gradient,
        summed[0],
        summed[1],
        summed[2],
        summed[3],
        query_gain_sum,
        key_gain_sum,
        summed[4],
        summed[5],
        summed[6],
        summed[7],
        summed[8],
    )


def solution(mesh):
    return jax.shard_map(
        per_device,
        mesh=mesh,
        in_specs=(
            P("dp", "row"),
            P("dp", None),
            P("row"),
            P("row", "col"),
            P("row", "col"),
            P("row", "col"),
            P(),
            P(),
            P("col", "row"),
            P("row"),
            P("row", "col"),
            P("row", "col"),
            P("col", "row"),
            P("dp", "row"),
        ),
        out_specs=(
            P("dp", "row"),
            P("dp", "row"),
            P("row"),
            P("row", "col"),
            P("row", "col"),
            P("row", "col"),
            P(),
            P(),
            P("col", "row"),
            P("row"),
            P("row", "col"),
            P("row", "col"),
            P("col", "row"),
        ),
        check_vma=False,
    )
```

profile of v0, /device:TPU:0, one launch (start us, length us, event | category | flops | bytes accessed | tf_op | source)
XLA Modules:
  0.0 995.9 jit_solution(13486363195298392930)
XLA Ops:
  8.6 11.4 %psum.133 = f32[384,1]{0,1:T(1,128)S(1)} all-reduce(f32[384,1]{0,1:T(1,128)S(1)} %broadcast_in_dim.30), channel_id=1, replica_groups=mesh['dp'=4,'row'=4,'col'=2] {'row'}, use_global_device_ids=true, to_apply=%region_1.2 | all-reduce | flops 384 | bytes 3072 | tf_op jit(solution)/shard_map/psum | solution.py:40
  39.3 37.8 %reduce-scatter.5.cloned.1.call-done = f32[384,512]{1,0:T(8,128)} async-done(((f32[384,2048]{1,0:T(8,128)}), f32[384,512]{1,0:T(8,128)}) %reduce-scatter.5.cloned.1.call-update) | async-done | bytes 786448 | tf_op jit(solution)/shard_map/reduce_scatter | solution.py:68
  112.1 11.1 %all_gather.14 = bf16[384,1024]{0,1:T(8,128)(2,1)S(1)} all-gather(bf16[384,256]{0,1:T(8,128)(2,1)S(1)} %bitcast.179), channel_id=1, replica_groups=mesh['dp'=4,'row'=4,'col'=2] {'row'}, dimensions={1}, use_global_device_ids=true | all-gather | bytes 983040 | tf_op jit(solution)/shard_map/all_gather | solution.py:73
  125.6 4.6 fusion.66
  130.5 6.8 reshape.452
  137.3 6.8 reshape.453
  144.1 8.4 pad_maximum_fusion
  152.5 7.4 copy.150
  162.5 10.1 %psum.135 = f32[384,1]{0,1:T(1,128)} all-reduce(f32[384,1]{0,1:T(1,128)} %broadcast_in_dim.34), channel_id=1, replica_groups=mesh['dp'=4,'row'=4,'col'=2] {'row'}, use_global_device_ids=true, to_apply=%region_10.11 | all-reduce | flops 384 | bytes 3072 | tf_op jit(solution)/shard_map/psum | solution.py:40
  173.3 9.4 fusion.58
  182.8 23.9 %reduce-scatter.9.cloned.1.call-done = f32[384,768]{1,0:T(8,128)} async-done(((f32[384,3072]{1,0:T(8,128)}), f32[384,768]{1,0:T(8,128)}) %reduce-scatter.9.cloned.1.call-update) | async-done | bytes 1179664 | tf_op jit(solution)/shard_map/reduce_scatter | solution.py:80
  206.7 97.9 %reduce-scatter.7.cloned.1.call-done = f32[384,1536]{1,0:T(8,128)} async-done(((f32[384,6144]{1,0:T(8,128)}), f32[384,1536]{1,0:T(8,128)}) %reduce-scatter.7.cloned.1.call-update) | async-done | bytes 2359312 | tf_op jit(solution)/shard_map/reduce_scatter | solution.py:68
  304.6 3.4 multiply_convert_fusion.1
  309.4 56.8 %all-gather.6.cloned.1.call-done = bf16[384,6144]{1,0:T(8,128)(2,1)} async-done(((bf16[384,1536]{1,0:T(8,128)(2,1)}), bf16[384,6144]{1,0:T(8,128)(2,1)}) %all-gather.6.cloned.1.call-update) | async-done | bytes 4718608 | tf_op jit(solution)/shard_map/all_gather | solution.py:93
  366.2 7.7 fusion.67
  374.0 19.1 %all-reduce.15.cloned.1.call-done = f32[384,512]{1,0:T(8,128)} async-done(((f32[384,512]{1,0:T(8,128)}), f32[384,512]{1,0:T(8,128)}) %all-reduce.15.cloned.1.call-update) | async-done | bytes 786448 | tf_op jit(solution)/shard_map/psum | solution.py:44
  395.4 10.8 %psum.138 = f32[384]{0:T(512)} all-reduce(f32[384]{0:T(512)} %get-tuple-element.14), channel_id=1, replica_groups=mesh['dp'=4,'row'=4,'col'=2] {'row'}, use_global_device_ids=true, to_apply=%region_16.17 | all-reduce | flops 384 | bytes 3072 | tf_op jit(solution)/shard_map/psum | solution.py:40
  411.5 29.6 %reduce-scatter.11.cloned.1.call-done = f32[384,256]{1,0:T(8,128)} async-done(((f32[384,1024]{1,0:T(8,128)}), f32[384,256]{1,0:T(8,128)}) %reduce-scatter.11.cloned.1.call-update) | async-done | bytes 393232 | tf_op jit(solution)/shard_map/reduce_scatter | solution.py:80
  459.8 21.1 %all-gather.4.cloned.1.call-done = bf16[384,3072]{1,0:T(8,128)(2,1)} async-done(((bf16[384,768]{1,0:T(8,128)(2,1)}), bf16[384,3072]{1,0:T(8,128)(2,1)}) %all-gather.4.cloned.1.call-update) | async-done | bytes 2359312 | tf_op jit(solution)/shard_map/all_gather | solution.py:73
  480.9 5.4 convolution_convert_fusion.1
  488.6 8.1 convolution_convert_fusion
  496.6 13.5 %reshape.465 = bf16[512,4,1536]{2,1,0:T(4,128)(2,1)} reshape(bf16[512,6144]{1,0:T(8,128)(2,1)} %convolution_convert_fusion) | data formatting | bytes 12582912 | tf_op jit(solution)/shard_map/convert.2
  510.2 4.0 all-gather.8.cloned.1.call-done
  514.2 3.3 fusion.68
  517.6 4.6 fusion.59
  537.4 45.1 %all-reduce.4 = (f32[128]{0:T(128)}, f32[128]{0:T(128)}) all-reduce(f32[128]{0:T(128)S(1)} %copy-done.52, f32[128]{0:T(128)S(1)} %copy-done.51), channel_id=1, replica_groups=mesh['dp'=4,'row'=4,'col'=2] {'dp','row','col'}, use_global_device_ids=true, to_apply=%region_30.31 | all-reduce | flops 256 | bytes 2048 | tf_op jit(solution)/shard_map/psum | solution.py:287
  584.1 10.7 %all-reduce.6 = (bf16[512]{0:T(512)(128)(2,1)S(1)}, bf16[512]{0:T(512)(128)(2,1)S(1)}) all-reduce(bf16[512]{0:T(512)(128)(2,1)S(1)} %get-tuple-element.15, bf16[512]{0:T(512)(128)(2,1)S(1)} %copy-done.50), channel_id=1, replica_groups=mesh['dp'=4,'row'=4,'col'=2] {'dp'}, use_global_device_ids=true, to_apply=%region_25.26 | all-reduce | flops 1024 | bytes 4096 | tf_op jit(solution)/shard_map/psum | solution.py:289
  596.0 9.8 psum.140
  608.9 362.6 %all-reduce.19.cloned.1.call-done = (bf16[512,1024]{1,0:T(8,128)(2,1)}, bf16[512,512]{1,0:T(8,128)(2,1)}, bf16[512,512]{1,0:T(8,128)(2,1)}, bf16[1024,512]{1,0:T...) async-done(((bf16[512,1024]{1,0:T(8,128)(2,1)}, bf16[512,512]{1,0:T(8,128)(2,1)}, bf16[512,512]{1,0:T(8,128)(2,1)}, ...) | async-done | bytes 12582928 | tf_op jit(solution)/shard_map/psum | solution.py:290
  978.2 3.5 convert_element_type.214
  981.7 3.5 convert_element_type.216
  985.3 3.6 convert_element_type.218
  (223 shorter events, 119.2 us)
Async XLA Ops:
  7.2 118.4 %copy-start = (bf16[3072,512]{1,0:T(8,128)(2,1)S(1)}, bf16[3072,512]{1,0:T(8,128)(2,1)}, u32[]{:S(2)}) copy-start(bf16[3072,512]{1,0:T(8,128)(2,1)} %param.26) | copy-start | bytes 9437188
  7.2 69.9 %reduce-scatter.5.cloned.1.call-start = ((), (), s32[]{:S(2)}) async-start(), calls=%async_computation.4 | async-start | bytes 3932160 | tf_op jit(solution)/shard_map/reduce_scatter | solution.py:68
  33.7 126.2 %all-reduce.13.cloned.1.call-start = ((), (), s32[]{:S(2)}) async-start(), calls=%async_computation.5 | async-start | bytes 1572864 | tf_op jit(solution)/shard_map/psum | solution.py:44
  38.4 48.8 %copy-start.47 = (f32[128]{0:T(128)S(1)}, f32[128]{0:T(128)}, u32[]{:S(2)}) copy-start(f32[128]{0:T(128)} %param.21) | copy-start | bytes 1540
  85.9 9.1 copy-start.43
  86.0 12.0 %copy-start.40 = (f32[384]{0:T(512)}, f32[384]{0:T(512)S(1)}, u32[]{:S(2)}) copy-start(f32[384]{0:T(512)S(1)} %fusion.57) | copy-start | bytes 4612
  98.0 11.2 %copy-start.42 = (f32[384,2]{0,1:T(2,128)}, f32[384,2]{0,1:T(2,128)S(1)}, u32[]{:S(2)}) copy-start(f32[384,2]{0,1:T(2,128)S(1)} %copy.113) | copy-start | bytes 9220
  109.2 16.4 %copy-start.46 = (f32[2,384]{1,0:T(2,128)}, f32[2,384]{1,0:T(2,128)S(1)}, u32[]{:S(2)}) copy-start(f32[2,384]{1,0:T(2,128)S(1)} %get-tuple-element.58) | copy-start | bytes 9220
  109.2 14.9 %copy-start.31 = (bf16[1024,512]{1,0:T(8,128)(2,1)S(1)}, bf16[1024,512]{1,0:T(8,128)(2,1)}, u32[]{:S(2)}) copy-start(bf16[1024,512]{1,0:T(8,128)(2,1)} %param.22) | copy-start | bytes 3145732
  125.6 81.1 %reduce-scatter.9.cloned.1.call-start = ((), (), s32[]{:S(2)}) async-start(), calls=%async_computation.8 | async-start | bytes 5898240 | tf_op jit(solution)/shard_map/reduce_scatter | solution.py:80
  130.3 174.3 %reduce-scatter.7.cloned.1.call-start = ((), (), s32[]{:S(2)}) async-start(), calls=%async_computation.6 | async-start | bytes 11796480 | tf_op jit(solution)/shard_map/reduce_scatter | solution.py:68
  152.5 20.9 %copy-start.37 = (f32[512]{0:T(512)S(1)}, f32[512]{0:T(512)}, u32[]{:S(2)}) copy-start(f32[512]{0:T(512)} %param.23) | copy-start | bytes 6148
  182.8 183.5 %all-gather.6.cloned.1.call-start = ((), (), s32[]{:S(2)}) async-start(), calls=%async_computation.9 | async-start | bytes 5898240 | tf_op jit(solution)/shard_map/all_gather | solution.py:93
  309.2 83.9 %all-reduce.15.cloned.1.call-start = ((), (), s32[]{:S(2)}) async-start(), calls=%async_computation.10 | async-start | bytes 1572864 | tf_op jit(solution)/shard_map/psum | solution.py:44
  374.0 67.1 %reduce-scatter.11.cloned.1.call-start = ((), (), s32[]{:S(2)}) async-start(), calls=%async_computation.11 | async-start | bytes 1966080 | tf_op jit(solution)/shard_map/reduce_scatter | solution.py:80
  410.7 70.2 %all-gather.4.cloned.1.call-start = ((), (), s32[]{:S(2)}) async-start(), calls=%async_computation.7 | async-start | bytes 2949120 | tf_op jit(solution)/shard_map/all_gather | solution.py:73
  411.5 102.7 %all-gather.8.cloned.1.call-start = ((), (), s32[]{:S(2)}) async-start(), calls=%async_computation.12 | async-start | bytes 1966080 | tf_op jit(solution)/shard_map/all_gather | solution.py:93
  454.5 3.7 copy-start.13
  454.5 3.7 copy-start.33
  454.5 4.0 copy-start.49
  459.5 123.0 %all-reduce.17.cloned.1.call-start = ((), (), s32[]{:S(2)}) async-start(), calls=%async_computation.13 | async-start | bytes 3145728 | tf_op jit(solution)/shard_map/psum | solution.py:44
  480.9 5.4 copy-start.53
  496.6 17.6 %copy-start.9 = (bf16[64,8,4,512]{3,1,2,0:T(8,128)(2,1)S(1)}, bf16[64,8,4,512]{3,1,2,0:T(8,128)(2,1)}, u32[]{:S(2)}) copy-start(bf16[64,8,4,512]{3,1,2,0:T(8,128)(2,1)} %copy-done.8) | copy-start | bytes 6291460
  517.5 454.0 %all-reduce.19.cloned.1.call-start = ((), (), s32[]{:S(2)}) async-start(), calls=%async_computation.14 | async-start | bytes 25165824 | tf_op jit(solution)/shard_map/psum | solution.py:290
  536.8 47.3 %copy-start.50 = (bf16[512]{0:T(512)(128)(2,1)S(1)}, bf16[512]{0:T(512)(128)(2,1)}, u32[]{:S(2)}) copy-start(bf16[512]{0:T(512)(128)(2,1)} %get-tuple-element.13) | copy-start | bytes 3076
  536.8 69.0 %copy-start.3 = (f32[384,512]{1,0:T(8,128)S(1)}, f32[384,512]{1,0:T(8,128)}, u32[]{:S(2)}) copy-start(f32[384,512]{1,0:T(8,128)} %get-tuple-element.37) | copy-start | bytes 2359300
  536.8 71.0 %copy-start.7 = (f32[384,512]{1,0:T(8,128)S(1)}, f32[384,512]{1,0:T(8,128)}, u32[]{:S(2)}) copy-start(f32[384,512]{1,0:T(8,128)} %copy-done.5) | copy-start | bytes 2359300
  582.5 25.2 %copy-start.23 = (f32[384,512]{1,0:T(8,128)S(1)}, f32[384,512]{1,0:T(8,128)}, u32[]{:S(2)}) copy-start(f32[384,512]{1,0:T(8,128)} %get-tuple-element.24) | copy-start | bytes 2359300
  971.5 4.0 copy-start.34
  978.2 3.5 copy-start.19
  981.7 3.5 copy-start.18
  985.2 3.6 copy-start.1
  (34 other events, 59.0 us)
Sparse Core Ops, SparseCore 0:
  33.8 43.2 reduce-scatter.4
  125.7 18.9 all-reduce.12
  148.2 58.4 reduce-scatter.8
  209.7 94.8 reduce-scatter.6
  309.3 56.9 all-gather.5
  374.1 18.9 all-reduce.14
  410.8 30.1 reduce-scatter.10
  443.5 37.3 all-gather.3
  483.3 30.8 all-gather.7
  517.7 20.4 all-reduce.16
  542.7 428.7 all-reduce.18
where the time goes:
time: 1000 us; the launch traced here: 996 us
  waiting for transfers between devices  654 us (65%)
  blocking collectives  109 us (11%)
  local copies, waits for them, and re-layouts  90.2 us (9%)
  other arithmetic  69.5 us (7%)
  matrix products  57.5 us (6%)
  between operations  14.9 us (1%)
    psum x1, waiting for transfers between devices, per_device(): lax.psum(query_sum.astype(jnp.bfloat16), 'dp').astype(jnp.float32)  363 us
    reduce_scatter x2, waiting for transfers between devices, project_in(): return lax.psum_scatter(partial_sum, 'row', scatter_dimension=1, tiled=True)  136 us
    all_gather x2, waiting for transfers between devices, input_gradients(): piece = lax.all_gather(local, 'row', axis=1, tiled=True)  60.8 us
    reduce_scatter x2, waiting for transfers between devices, project_back(): return lax.psum_scatter(partial_sum, 'row', scatter_dimension=1, tiled=True)  53.5 us
    psum x1, blocking collectives, per_device(): lax.psum((query_gain_back, key_gain_back), ('dp', 'row', 'col'))  45.1 us
    psum x4, blocking collectives, width_total(): return lax.psum(jnp.sum(values, axis=1, keepdims=True), 'row')  42.1 us
    all_gather x1, waiting for transfers between devices, project_out(): lax.all_gather(local, 'row', axis=1, tiled=True)  21.1 us
    unnamed x113, local copies, waits for them, and re-layouts  20.3 us
  transfers between devices with their start and end apart: 11, of which 9 were waited for; matrix products, arithmetic and copies ran while one was open for 12% of the time, Pallas kernels for 0%

commit v1 on v0

v1 whole, which is shorter than its diff:
```python
from functools import partial

import jax
import jax.numpy as jnp
from jax import lax
from jax.experimental import pallas as pl
from jax.experimental.pallas import tpu as pltpu
from jax.sharding import PartitionSpec as P

epsilon = 1e-06
rope_base = 1000000.0
lanes = 128
full_vmem = 67043328
chunk_limit = 262144
low = jnp.bfloat16
wide = jnp.float32


def dot(a, b, contract=((1,), (0,))):
    return lax.dot_general(a, b, (contract, ((), ())), preferred_element_type=wide)


def dot_t(a, b):
    return dot(a, b, ((1,), (1,)))


def t_dot(a, b):
    return dot(a, b, ((0,), (0,)))


def window(index, size):
    return pl.ds(pl.multiple_of(index * size, lanes), size)


def remote(source, target, send, receive, axis, index):
    return pltpu.make_async_remote_copy(
        src_ref=source,
        dst_ref=target,
        send_sem=send,
        recv_sem=receive,
        device_id={axis: index},
        device_id_type=pl.DeviceIdType.MESH,
    )


def greet(groups):
    barrier = pltpu.get_barrier_semaphore()
    total = 0
    for axis, size in groups:
        me = lax.axis_index(axis)
        for shift in range(1, size):
            pl.semaphore_signal(
                barrier,
                inc=1,
                device_id={axis: lax.rem(me + shift, size)},
                device_id_type=pl.DeviceIdType.MESH,
            )
            total += 1
    if total:
        pl.semaphore_wait(barrier, total)


def half_turn(values):
    size = values.shape[-1]
    turned = pltpu.roll(values, size // 2, axis=1)
    lane = lax.broadcasted_iota(jnp.int32, values.shape, 1)
    return jnp.where(lane < size // 2, -turned, turned)


class Exchange:
    def __init__(self, axis, size, send, receive, send_sem, receive_sem):
        self.axis, self.size = axis, size
        self.send, self.receive = send, receive
        self.send_sem, self.receive_sem = send_sem, receive_sem
        self.me = lax.axis_index(axis)

    def target(self, shift):
        return lax.rem(self.me + shift, self.size)

    def source(self, shift):
        return lax.rem(self.me + self.size - shift, self.size)

    def copy(self, shift):
        sent = self.send(shift)
        return remote(
            sent,
            self.receive.at[shift - 1],
            self.send_sem.at[shift - 1],
            self.receive_sem.at[shift - 1],
            self.axis,
            self.target(shift),
        )

    def start(self, shift):
        self.copy(shift).start()

    def arrive(self, shift):
        self.copy(shift).wait_recv()

    def finish(self):
        for shift in range(1, self.size):
            self.copy(shift).wait_send()


class Ranked(Exchange):
    def copy(self, shift):
        return remote(
            self.send(shift),
            self.receive.at[self.me],
            self.send_sem.at[shift - 1],
            self.receive_sem.at[shift - 1],
            self.axis,
            self.target(shift),
        )

    def total(self, rows):
        result = self.receive[0, rows]
        for member in range(1, self.size):
            result = result + self.receive[member, rows]
        return result


def each_tile(rows, body):
    tile = lanes if rows % lanes == 0 else rows

    def step(index, carry):
        body(pl.ds(pl.multiple_of(index * tile, tile), tile), index * tile, tile)
        return carry

    lax.fori_loop(0, rows // tile, step, 0)


def forward_kernel(
    rows_of,
    cols_of,
    x,
    seg_row,
    seg_col,
    inverse,
    gain1,
    wq,
    wk,
    wv,
    qn,
    kn,
    wo,
    gain2,
    wg,
    wu,
    wd,
    ct,
    n1,
    fs,
    raw,
    lows,
    shares,
    trig,
    mixed,
    mid,
    ss,
    n2,
    hid,
    gub,
    unit,
    pq_own,
    pq_s,
    pq_r,
    ph_own,
    ph_s,
    ph_r,
    pg_own,
    pg_s,
    pg_r,
    mixed_r,
    stat_s,
    stat_r,
    ox_s,
    ox_r,
    row_send,
    row_recv,
    stat_send,
    stat_recv,
    col_send,
    col_recv,
):
    tokens, depth = x.shape
    width = depth * rows_of
    qw, kw, fw = wq.shape[1] // rows_of, wk.shape[1] // rows_of, wg.shape[1] // rows_of
    size = qn.shape[1]
    heads, key_heads = qw // size, kw // size
    group = heads // key_heads
    scale = size ** (-0.5)
    me = lax.axis_index("row")
    greet((("row", rows_of), ("col", cols_of)))

    def row_exchange(kind, send, receive):
        return Exchange("row", rows_of, send, receive, row_send.at[kind], row_recv.at[kind])

    def stat_exchange(kind):
        return Ranked(
            "row",
            rows_of,
            lambda shift: stat_s.at[kind],
            stat_r.at[kind],
            stat_send.at[kind],
            stat_recv.at[kind],
        )

    stat1 = stat_exchange(0)

    def prepare(rows, start, tile):
        value = x[rows, :].astype(wide)
        square = jnp.broadcast_to(jnp.sum(value * value, axis=1, keepdims=True), (tile, lanes))
        stat_s[0, rows] = square
        stat_r[0, me, rows] = square
        unit[rows, :] = (value * gain1[...]).astype(low)

    each_tile(tokens, prepare)
    for shift in range(1, rows_of):
        stat1.start(shift)

    def project(index, target, slot):
        u = unit[...]
        q = dot(u, wq[:, window(index, qw)])
        k = dot(u, wk[:, window(index, kw)])
        v = dot(u, wv[:, window(index, kw)])
        kind = target.dtype
        if slot is None:
            target[:, :qw] = q.astype(kind)
            target[:, qw : qw + kw] = k.astype(kind)
            target[:, qw + kw :] = v.astype(kind)
        else:
            target[slot, :, :qw] = q.astype(kind)
            target[slot, :, qw : qw + kw] = k.astype(kind)
            target[slot, :, qw + kw :] = v.astype(kind)

    qkv = row_exchange(0, lambda shift: pq_s.at[shift - 1], pq_r)
    for shift in range(1, rows_of):
        project(qkv.target(shift), pq_s, shift - 1)
        qkv.start(shift)
    project(me, pq_own, None)

    back = row_exchange(1, lambda shift: ph_s.at[shift - 1], ph_r)
    for shift in range(1, rows_of):
        ph_s[shift - 1] = dot_t(ct[...], wd[window(back.target(shift), fw), :]).astype(low)
        back.start(shift)
    ph_own[...] = dot_t(ct[...], wd[window(me, fw), :])

    def tables(rows, start, tile):
        key = lax.broadcasted_iota(jnp.int32, (tile, tokens), 1)
        query = lax.broadcasted_iota(jnp.int32, (tile, tokens), 0) + start
        allowed = (seg_col[rows, :] == seg_row[...]) & (key <= query)
        count = jnp.sum(jnp.where(allowed, 1.0, 0.0), axis=1, keepdims=True) - 1.0
        angle = count * inverse[...]
        trig[0, rows, :] = jnp.cos(angle)
        trig[1, rows, :] = jnp.sin(angle)

    each_tile(tokens, tables)

    for shift in range(1, rows_of):
        stat1.arrive(shift)
        qkv.arrive(shift)

    def heads_in(rows, start, tile):
        first = lax.rsqrt(stat1.total(rows) / width + epsilon)
        fs[rows, :] = first
        first = first[:, :1]
        n1[rows, :] = (x[rows, :].astype(wide) * first * gain1[...]).astype(low)
        value = pq_own[rows, :]
        for shift in range(1, rows_of):
            value = value + pq_r[shift - 1, rows, :].astype(wide)
        value = value * first
        raw[rows, :] = value[:, : qw + kw]
        cosine, sine = trig[0, rows, :], trig[1, rows, :]
        for head in range(heads + key_heads):
            piece = value[:, head * size : (head + 1) * size]
            gain = qn[...] if head < heads else kn[...]
            norm = lax.rsqrt(jnp.mean(piece * piece, axis=1, keepdims=True) + epsilon)
            normed = piece * norm * gain
            rotated = normed * cosine + half_turn(normed) * sine
            lows[rows, head * size : (head + 1) * size] = rotated.astype(low)
        lows[rows, qw + kw :] = value[:, qw + kw :].astype(low)

    each_tile(tokens, heads_in)

    def attend(rows, start, tile):
        key = lax.broadcasted_iota(jnp.int32, (tile, tokens), 1)
        query = lax.broadcasted_iota(jnp.int32, (tile, tokens), 0) + start
        allowed = (seg_col[rows, :] == seg_row[...]) & (key <= query)
        for head in range(heads):
            pair = head // group
            keys = lows[:, qw + pair * size : qw + (pair + 1) * size]
            values = lows[:, qw + kw + pair * size : qw + kw + (pair + 1) * size]
            scores = dot_t(lows[rows, head * size : (head + 1) * size], keys) * scale
            numerators = jnp.where(allowed, jnp.exp(scores), 0.0)
            share = numerators / jnp.sum(numerators, axis=1, keepdims=True)
            shares[head, rows, :] = share
            mixed[0, rows, head * size : (head + 1) * size] = dot(
                share.astype(low), values
            ).astype(low)

    each_tile(tokens, attend)

    gather = row_exchange(2, lambda shift: mixed.at[0], mixed_r)
    for shift in range(1, rows_of):
        gather.start(shift)
    ox_s[...] = dot(mixed[0], wo[window(me, qw), :])
    for shift in range(1, rows_of):
        gather.arrive(shift)
        mixed[shift] = mixed_r[shift - 1]
        ox_s[...] += dot(mixed_r[shift - 1], wo[window(gather.source(shift), qw), :])
    column = Exchange("col", cols_of, lambda shift: ox_s, ox_r, col_send, col_recv)
    for shift in range(1, cols_of):
        column.start(shift)
    for shift in range(1, cols_of):
        column.arrive(shift)

    stat2 = stat_exchange(1)

    def middle(rows, start, tile):
        value = ox_s[rows, :]
        for shift in range(1, cols_of):
            value = value + ox_r[shift - 1, rows, :]
        value = x[rows, :].astype(wide) + value
        mid[rows, :] = value
        square = jnp.broadcast_to(jnp.sum(value * value, axis=1, keepdims=True), (tile, lanes))
        stat_s[1, rows] = square
        stat_r[1, me, rows] = square
        unit[rows, :] = (value * gain2[...]).astype(low)

    each_tile(tokens, middle)
    for shift in range(1, rows_of):
        stat2.start(shift)

    feed = row_exchange(3, lambda shift: pg_s.at[shift - 1], pg_r)
    for shift in range(1, rows_of):
        columns = window(feed.target(shift), fw)
        pg_s[shift - 1, :, :fw] = dot(unit[...], wg[:, columns]).astype(low)
        pg_s[shift - 1, :, fw:] = dot(unit[...], wu[:, columns]).astype(low)
        feed.start(shift)
    pg_own[:, :fw] = dot(unit[...], wg[:, window(me, fw)])
    pg_own[:, fw:] = dot(unit[...], wu[:, window(me, fw)])
    for shift in range(1, rows_of):
        stat2.arrive(shift)
        back.arrive(shift)

    def scale_rows(rows, start, tile):
        second = lax.rsqrt(stat2.total(rows) / width + epsilon)
        ss[rows, :] = second
        n2[rows, :] = (mid[rows, :] * second[:, :1] * gain2[...]).astype(low)

    each_tile(tokens, scale_rows)
    for shift in range(1, rows_of):
        feed.arrive(shift)

    def activate(rows, start, tile):
        second = ss[rows, :1]
        gate = pg_own[rows, :fw]
        upward = pg_own[rows, fw:]
        for shift in range(1, rows_of):
            gate = gate + pg_r[shift - 1, rows, :fw].astype(wide)
            upward = upward + pg_r[shift - 1, rows, fw:].astype(wide)
        gate = gate * second
        upward = upward * second
        behind = ph_own[rows, :]
        for shift in range(1, rows_of):
            behind = behind + ph_r[shift - 1, rows, :].astype(wide)
        sigmoid = jax.nn.sigmoid(gate)
        silu = gate * sigmoid
        hid[rows, :] = (silu * upward).astype(low)
        gub[rows, :fw] = (behind * upward * sigmoid * (1.0 + gate * (1.0 - sigmoid))).astype(low)
        gub[rows, fw:] = (behind * silu).astype(low)

    each_tile(tokens, activate)
    for exchange in (stat1, qkv, back, gather, column, stat2, feed):
        exchange.finish()


def backward_kernel(
    rows_of,
    cols_of,
    x,
    ct,
    n1,
    fs,
    raw,
    lows,
    shares,
    trig,
    mixed,
    mid,
    ss,
    n2,
    hid,
    gub,
    gain1,
    gain2,
    qn,
    kn,
    wq,
    wk,
    wv,
    wo,
    wg,
    wu,
    wd,
    bo,
    ig,
    small,
    gq,
    gk,
    gv,
    go,
    gg,
    gu,
    gd,
    hid_r,
    gub_r,
    n_t,
    mb,
    ml,
    pm_own,
    pm_s,
    pm_r,
    sl,
    sb,
    dqkv,
    dqkv_r,
    gains,
    stat_s,
    stat_r,
    ox_s,
    ox_r,
    row_send,
    row_recv,
    stat_send,
    stat_recv,
    col_send,
    col_recv,
):
    tokens, depth = x.shape
    width = depth * rows_of
    qw, kw, fw = wq.shape[1] // rows_of, wk.shape[1] // rows_of, wg.shape[1] // rows_of
    size = qn.shape[1]
    heads, key_heads = qw // size, kw // size
    group = heads // key_heads
    scale = size ** (-0.5)
    me = lax.axis_index("row")
    greet((("row", rows_of), ("col", cols_of)))

    def row_exchange(kind, send, receive):
        return Exchange("row", rows_of, send, receive, row_send.at[kind], row_recv.at[kind])

    def stat_exchange(kind):
        return Ranked(
            "row",
            rows_of,
            lambda shift: stat_s.at[kind],
            stat_r.at[kind],
            stat_send.at[kind],
            stat_recv.at[kind],
        )

    def column_exchange(kind):
        return Exchange(
            "col",
            cols_of,
            lambda shift: ox_s.at[kind],
            ox_r.at[kind],
            col_send.at[kind],
            col_recv.at[kind],
        )

    def column_sum(kind, rows):
        value = ox_s[kind, rows, :]
        for shift in range(1, cols_of):
            value = value + ox_r[kind, shift - 1, rows, :]
        return value

    hide = row_exchange(0, lambda shift: hid, hid_r)
    gates = row_exchange(1, lambda shift: gub, gub_r)
    for shift in range(1, rows_of):
        hide.start(shift)
    for shift in range(1, rows_of):
        gates.start(shift)
    body = pl.ds(0, tokens)
    cut = ct[...]
    for shift in range(rows_of):
        if shift:
            hide.arrive(shift)
        piece = hid[...] if shift == 0 else hid_r[shift - 1]
        index = window(hide.source(shift), fw)
        part = dot(piece, wd[index, :])
        if shift == 0:
            ox_s[0, body, :] = part
        else:
            ox_s[0, body, :] += part
        gd[index, :] = t_dot(piece, cut).astype(low)
    column0 = column_exchange(0)
    for shift in range(1, cols_of):
        column0.start(shift)
    n_t[...] = n2[...].T
    for shift in range(rows_of):
        if shift:
            gates.arrive(shift)
        piece = gub if shift == 0 else gub_r.at[shift - 1]
        index = window(gates.source(shift), fw)
        part = dot_t(piece[:, :fw], wg[:, index]) + dot_t(piece[:, fw:], wu[:, index])
        if shift == 0:
            ox_s[1, body, :] = part
        else:
            ox_s[1, body, :] += part
    column1 = column_exchange(1)
    for shift in range(1, cols_of):
        column1.start(shift)
    for shift in range(1, cols_of):
        column0.arrive(shift)

    def result(rows, start, tile):
        bo[rows, :] = (mid[rows, :] + column_sum(0, rows)).astype(low)

    each_tile(tokens, result)
    for shift in range(1, cols_of):
        column1.arrive(shift)

    stat2 = stat_exchange(0)
    small[...] = jnp.zeros_like(small)
    gains[...] = jnp.zeros_like(gains)

    def feed_stat(rows, start, tile):
        back = column_sum(1, rows)
        unit = mid[rows, :] * ss[rows, :1]
        small[1:2, :] += jnp.sum(back * unit, axis=0, keepdims=True)
        inner = jnp.sum(back * gain2[...] * unit, axis=1, keepdims=True)
        inner = jnp.broadcast_to(inner, (tile, lanes))
        stat_s[0, rows] = inner
        stat_r[0, me, rows] = inner

    each_tile(tokens, feed_stat)
    pad = pl.ds(tokens, 8)
    stat_s[0, pad] = jnp.zeros((8, lanes), wide)
    for shift in range(1, rows_of):
        stat2.start(shift)
    for shift in range(rows_of):
        piece = gub if shift == 0 else gub_r.at[shift - 1]
        index = window(gates.source(shift), fw)
        gg[:, index] = dot(n_t[...], piece[:, :fw]).astype(low)
    for shift in range(1, rows_of):
        stat2.arrive(shift)

    def middle_back(rows, start, tile):
        second = ss[rows, :1]
        unit = mid[rows, :] * second
        inner = stat2.total(rows)[:, :1] / width
        value = ct[rows, :].astype(wide) + second * (
            column_sum(1, rows) * gain2[...] - unit * inner
        )
        mb[rows, :] = value
        ml[rows, :] = value.astype(low)

    each_tile(tokens, middle_back)
    blend = row_exchange(2, lambda shift: pm_s.at[shift - 1], pm_r)
    for shift in range(1, rows_of):
        pm_s[shift - 1] = dot_t(ml[...], wo[window(blend.target(shift), qw), :]).astype(low)
        blend.start(shift)
    pm_own[...] = dot_t(ml[...], wo[window(me, qw), :])
    for shift in range(rows_of):
        index = window(blend.source(shift), qw)
        go[index, :] = t_dot(mixed[shift], ml[...]).astype(low)
    for shift in range(1, rows_of):
        blend.arrive(shift)

    def share_back(rows, start, tile):
        value = pm_own[rows, :]
        for shift in range(1, rows_of):
            value = value + pm_r[shift - 1, rows, :].astype(wide)
        incoming = value.astype(low)
        pm_s[0, rows, :] = incoming
        product = incoming.astype(wide) * mixed[0, rows, :].astype(wide)
        for head in range(heads):
            pair = head // group
            part = slice(head * size, (head + 1) * size)
            values = lows[:, qw + kw + pair * size : qw + kw + (pair + 1) * size]
            delta = jnp.sum(product[:, part], axis=1, keepdims=True)
            share = shares[head, rows, :]
            sl[head, rows, :] = share.astype(low)
            sb[head, rows, :] = (share * (dot_t(incoming[:, part], values) - delta)).astype(low)

    blend.finish()
    each_tile(tokens, share_back)
    n_t[...] = n1[...].T

    def pull(head, back, gain, row):
        raw_piece = raw[:, head * size : (head + 1) * size]
        norm = lax.rsqrt(jnp.mean(raw_piece * raw_piece, axis=1, keepdims=True) + epsilon)
        unit = raw_piece * norm
        normed_back = back * trig[0] - half_turn(back * trig[1])
        gains[row : row + 1, :] += jnp.sum(normed_back * unit, axis=0, keepdims=True)
        unit_back = normed_back * gain
        return norm * (unit_back - unit * jnp.mean(unit_back * unit, axis=1, keepdims=True))

    for pair in range(key_heads):
        keys = lows[:, qw + pair * size : qw + (pair + 1) * size]
        key_back = jnp.zeros((tokens, size), wide)
        value_back = jnp.zeros((tokens, size), wide)
        for head in range(pair * group, (pair + 1) * group):
            part = slice(head * size, (head + 1) * size)
            value_back = value_back + t_dot(sl[head], pm_s[0, :, part])
            key_back = key_back + scale * t_dot(sb[head], lows[:, part])
            query_back = scale * dot(sb[head], keys)
            dqkv[:, part] = pull(head, query_back, qn[...], 0).astype(low)
        spot = qw + pair * size
        dqkv[:, spot : spot + size] = pull(heads + pair, key_back, kn[...], 1).astype(low)
        spot = qw + kw + pair * size
        dqkv[:, spot : spot + size] = value_back.astype(low)

    deliver = row_exchange(3, lambda shift: dqkv, dqkv_r)
    for shift in range(1, rows_of):
        deliver.start(shift)
    for shift in range(rows_of):
        if shift:
            deliver.arrive(shift)
        piece = dqkv if shift == 0 else dqkv_r.at[shift - 1]
        source = deliver.source(shift)
        part = dot_t(piece[:, :qw], wq[:, window(source, qw)])
        part = part + dot_t(piece[:, qw : qw + kw], wk[:, window(source, kw)])
        part = part + dot_t(piece[:, qw + kw :], wv[:, window(source, kw)])
        if shift == 0:
            ox_s[2, body, :] = part
        else:
            ox_s[2, body, :] += part
    ox_s[2, pad, :] = jnp.zeros((8, depth), wide)
    ox_s[2, pad, :lanes] = gains[...]
    column2 = column_exchange(2)
    for shift in range(1, cols_of):
        column2.start(shift)
    for shift in range(rows_of):
        piece = dqkv if shift == 0 else dqkv_r.at[shift - 1]
        source = deliver.source(shift)
        gq[:, window(source, qw)] = dot(n_t[...], piece[:, :qw]).astype(low)
        gk[:, window(source, kw)] = dot(n_t[...], piece[:, qw : qw + kw]).astype(low)
        gv[:, window(source, kw)] = dot(n_t[...], piece[:, qw + kw :]).astype(low)
    for shift in range(1, cols_of):
        column2.arrive(shift)

    stat1 = stat_exchange(1)

    def first_stat(rows, start, tile):
        back = column_sum(2, rows)
        unit = x[rows, :].astype(wide) * fs[rows, :1]
        small[0:1, :] += jnp.sum(back * unit, axis=0, keepdims=True)
        inner = jnp.sum(back * gain1[...] * unit, axis=1, keepdims=True)
        inner = jnp.broadcast_to(inner, (tile, lanes))
        stat_s[1, rows] = inner
        stat_r[1, me, rows] = inner

    each_tile(tokens, first_stat)
    summed = column_sum(2, pad)[:, :lanes]
    stat_s[1, pad] = summed
    stat_r[1, me, pad] = summed
    for shift in range(1, rows_of):
        stat1.start(shift)
    n_t[...] = n2[...].T
    for shift in range(rows_of):
        piece = gub if shift == 0 else gub_r.at[shift - 1]
        index = window(gates.source(shift), fw)
        gu[:, index] = dot(n_t[...], piece[:, fw:]).astype(low)
    for shift in range(1, rows_of):
        stat1.arrive(shift)

    def finish(rows, start, tile):
        first = fs[rows, :1]
        unit = x[rows, :].astype(wide) * first
        inner = stat1.total(rows)[:, :1] / width
        ig[rows, :] = mb[rows, :] + first * (column_sum(2, rows) * gain1[...] - unit * inner)

    each_tile(tokens, finish)
    small[8:16, :lanes] = stat1.total(pad)
    for exchange in (hide, gates, column0, column1, stat2, deliver, column2, stat1):
        exchange.finish()


def chunks_of(shape):
    rows, columns = shape
    count = 1
    while rows % count or (rows // count) * columns > chunk_limit:
        count += 1
    return count, rows // count


def combine_kernel(members, shapes, *refs):
    count = len(shapes)
    small, *own = refs[: count + 1]
    small_out, *out = refs[count + 1 : 2 * count + 2]
    near = refs[2 * count + 2 : 3 * count + 2]
    far = refs[3 * count + 2 : 4 * count + 2]
    small_r, in_send, near_sem, far_sem, out_send, small_send, small_recv = refs[4 * count + 2 :]
    greet((("dp", members),))
    me = lax.axis_index("dp")
    half = members // 2
    left = me < half
    place = jnp.where(left, half - 1 - me, me - half)
    inner = jnp.where(left, me + 1, me - 1)
    outer = jnp.where(left, jnp.maximum(me - 1, 0), jnp.minimum(me + 1, members - 1))
    is_mid = place == 0
    has_outer = place < half - 1
    ranked = Ranked("dp", members, lambda shift: small, small_r, small_send, small_recv)
    small_r[me] = small[...]
    for shift in range(1, members):
        ranked.start(shift)

    bases, base = [], 0
    for shape in shapes:
        bases.append(base)
        base += chunks_of(shape)[0]

    def inward(which, index, source, target, target_sem):
        rows = chunks_of(shapes[which])[1]
        spot = pl.ds(pl.multiple_of(index * rows, 16), rows)
        slot = bases[which] + index
        return remote(
            source[which].at[spot],
            target[which].at[spot],
            in_send.at[slot],
            target_sem.at[slot],
            "dp",
            inner,
        )

    def outward(which, index):
        rows = chunks_of(shapes[which])[1]
        spot = pl.ds(pl.multiple_of(index * rows, 16), rows)
        slot = bases[which] + index
        return remote(
            out[which].at[spot],
            far[which].at[spot],
            out_send.at[slot],
            far_sem.at[slot],
            "dp",
            outer,
        )

    def add(which, index, first, second, target):
        rows = chunks_of(shapes[which])[1]
        spot = pl.ds(pl.multiple_of(index * rows, 16), rows)
        total = first[which][spot, :].astype(wide) + second[which][spot, :].astype(wide)
        target[which][spot, :] = total.astype(low)

    def send_in(which, index):
        target, sem = near, near_sem

        @pl.when(has_outer)
        def _():
            inward(which, index, near, near, near_sem).wait_recv()
            add(which, index, own, near, near)

            @pl.when(is_mid)
            def _():
                inward(which, index, near, far, far_sem).start()

            @pl.when(jnp.logical_not(is_mid))
            def _():
                inward(which, index, near, near, near_sem).start()

        @pl.when(jnp.logical_not(has_outer))
        def _():
            @pl.when(is_mid)
            def _():
                inward(which, index, own, far, far_sem).start()

            @pl.when(jnp.logical_not(is_mid))
            def _():
                inward(which, index, own, near, near_sem).start()

    def finish_chunk(which, index):
        inward(which, index, own, far, far_sem).wait_recv()

        @pl.when(is_mid)
        def _():
            @pl.when(has_outer)
            def _():
                add(which, index, near, far, out)

            @pl.when(jnp.logical_not(has_outer))
            def _():
                add(which, index, own, far, out)

        @pl.when(jnp.logical_not(is_mid))
        def _():
            rows = chunks_of(shapes[which])[1]
            spot = pl.ds(pl.multiple_of(index * rows, 16), rows)
            out[which][spot, :] = far[which][spot, :]

        @pl.when(has_outer)
        def _():
            outward(which, index).start()

    def over(which, body):
        def step(index, carry):
            body(index)
            return carry

        lax.fori_loop(0, chunks_of(shapes[which])[0], step, 0)

    @pl.when(is_mid)
    def _():
        for which in range(count):

            def both(index, which=which):
                send_in(which, index)

                @pl.when(index > 0)
                def _():
                    finish_chunk(which, index - 1)

            over(which, both)
            finish_chunk(which, chunks_of(shapes[which])[0] - 1)

    @pl.when(jnp.logical_not(is_mid))
    def _():
        for which in range(count):
            over(which, lambda index, which=which: send_in(which, index))
        for which in range(count):
            over(which, lambda index, which=which: finish_chunk(which, index))

    for shift in range(1, members):
        ranked.arrive(shift)
    result = small_r[0]
    for member in range(1, members):
        result = result + small_r[member]
    small_out[...] = result
    ranked.finish()
    for which in range(count):

        def drain(index, which=which):
            inward(which, index, own, near, near_sem).wait_send()

            @pl.when(has_outer)
            def _():
                outward(which, index).wait_send()

        over(which, drain)


def vmem(shape, kind):
    return pltpu.VMEM(shape, kind)


def call(kernel, shapes, scratch, identity, arguments):
    inside = pl.BlockSpec(memory_space=pltpu.VMEM)
    return pl.pallas_call(
        kernel,
        out_shape=tuple(jax.ShapeDtypeStruct(shape, kind) for shape, kind in shapes),
        in_specs=[inside] * len(arguments),
        out_specs=tuple([inside] * len(shapes)),
        scratch_shapes=scratch,
        compiler_params=pltpu.CompilerParams(
            collective_id=identity, has_side_effects=True, vmem_limit_bytes=full_vmem
        ),
    )(*arguments)


def per_device(
    block_input,
    segments,
    attention_norm,
    query_weight,
    key_weight,
    value_weight,
    query_norm,
    key_norm,
    output_weight,
    feedforward_norm,
    gate_weight,
    up_weight,
    down_weight,
    cotangent,
):
    rows_of, cols_of, members = (lax.axis_size(name) for name in ("row", "col", "dp"))
    tokens, depth = block_input.shape
    size = query_norm.shape[0]
    qw, kw, fw = (
        weight.shape[1] // rows_of for weight in (query_weight, key_weight, gate_weight)
    )
    heads = qw // size
    others, beside = max(rows_of - 1, 1), max(cols_of - 1, 1)
    half = size // 2
    inverse = rope_base ** (-2.0 * jnp.arange(half, dtype=wide) / size)
    inverse = jnp.concatenate([inverse, inverse])[None, :]
    seg_row = segments.reshape(1, tokens)
    seg_col = segments.reshape(tokens, 1)
    gain1, gain2 = attention_norm[None, :], feedforward_norm[None, :]
    qn, kn = query_norm[None, :], key_norm[None, :]
    total = qw + 2 * kw
    dma = pltpu.SemaphoreType.DMA

    def sems(kinds):
        return [
            dma((4, others)),
            dma((4, others)),
            dma((2, others)),
            dma((2, others)),
            dma((kinds, beside)) if kinds > 1 else dma((beside,)),
            dma((kinds, beside)) if kinds > 1 else dma((beside,)),
        ]

    saved = call(
        partial(forward_kernel, rows_of, cols_of),
        (
            ((tokens, depth), low),
            ((tokens, lanes), wide),
            ((tokens, qw + kw), wide),
            ((tokens, total), low),
            ((heads, tokens, tokens), wide),
            ((2, tokens, size), wide),
            ((rows_of, tokens, qw), low),
            ((tokens, depth), wide),
            ((tokens, lanes), wide),
            ((tokens, depth), low),
            ((tokens, fw), low),
            ((tokens, 2 * fw), low),
        ),
        [
            vmem((tokens, depth), low),
            vmem((tokens, total), wide),
            vmem((others, tokens, total), low),
            vmem((others, tokens, total), low),
            vmem((tokens, fw), wide),
            vmem((others, tokens, fw), low),
            vmem((others, tokens, fw), low),
            vmem((tokens, 2 * fw), wide),
            vmem((others, tokens, 2 * fw), low),
            vmem((others, tokens, 2 * fw), low),
            vmem((others, tokens, qw), low),
            vmem((2, tokens, lanes), wide),
            vmem((2, rows_of, tokens, lanes), wide),
            vmem((tokens, depth), wide),
            vmem((beside, tokens, depth), wide),
        ]
        + sems(1),
        0,
        (
            block_input,
            seg_row,
            seg_col,
            inverse,
            gain1,
            query_weight,
            key_weight,
            value_weight,
            qn,
            kn,
            output_weight,
            gain2,
            gate_weight,
            up_weight,
            down_weight,
            cotangent,
        ),
    )
    weights = (query_weight, key_weight, value_weight, output_weight, gate_weight, up_weight)
    shapes = [weight.shape for weight in weights] + [down_weight.shape]
    block_output, input_gradient, small, *partials = call(
        partial(backward_kernel, rows_of, cols_of),
        (
            ((tokens, depth), low),
            ((tokens, depth), wide),
            ((16, depth), wide),
            *((shape, low) for shape in shapes),
        ),
        [
            vmem((others, tokens, fw), low),
            vmem((others, tokens, 2 * fw), low),
            vmem((depth, tokens), low),
            vmem((tokens, depth), wide),
            vmem((tokens, depth), low),
            vmem((tokens, qw), wide),
            vmem((others, tokens, qw), low),
            vmem((others, tokens, qw), low),
            vmem((heads, tokens, tokens), low),
            vmem((heads, tokens, tokens), low),
            vmem((tokens, total), low),
            vmem((others, tokens, total), low),
            vmem((8, lanes), wide),
            vmem((2, tokens + 8, lanes), wide),
            vmem((2, rows_of, tokens + 8, lanes), wide),
            vmem((3, tokens + 8, depth), wide),
            vmem((3, beside, tokens + 8, depth), wide),
        ]
        + sems(3),
        1,
        (
            block_input,
            cotangent,
            *saved,
            gain1,
            gain2,
            qn,
            kn,
            *weights,
            down_weight,
        ),
    )
    if members > 1:
        slots = sum(chunks_of(shape)[0] for shape in shapes)
        small, *partials = call(
            partial(combine_kernel, members, shapes),
            (((16, depth), wide), *((shape, low) for shape in shapes)),
            [vmem(shape, low) for shape in shapes] * 2
            + [vmem((members, 16, depth), wide)]
            + [dma((slots,))] * 4
            + [dma((members - 1,))] * 2,
            2,
            (small, *partials),
        )
    gq, gk, gv, go, gg, gu, gd = (partial_sum.astype(wide) for partial_sum in partials)
    return (
        block_output,
        input_gradient,
        small[0],
        gq,
        gk,
        gv,
        small[8, :size],
        small[9, :size],
        go,
        small[1],
        gg,
        gu,
        gd,
    )


def solution(mesh):
    return jax.shard_map(
        per_device,
        mesh=mesh,
        in_specs=(
            P("dp", "row"),
            P("dp", None),
            P("row"),
            P("row", "col"),
            P("row", "col"),
            P("row", "col"),
            P(),
            P(),
            P("col", "row"),
            P("row"),
            P("row", "col"),
            P("row", "col"),
            P("col", "row"),
            P("dp", "row"),
        ),
        out_specs=(
            P("dp", "row"),
            P("dp", "row"),
            P("row"),
            P("row", "col"),
            P("row", "col"),
            P("row", "col"),
            P(),
            P(),
            P("col", "row"),
            P("row"),
            P("row", "col"),
            P("row", "col"),
            P("col", "row"),
        ),
        check_vma=False,
    )
```

time: 1000 us -> 629 us (0.63)
  waiting for transfers between devices: 654 us -> 0 us
  Pallas kernels: 0 us -> 604 us
  blocking collectives: 109 us -> 0 us
  local copies, waits for them, and re-layouts: 90.2 us -> 5.8 us
  matrix products: 57.5 us -> 0 us
  other arithmetic: 69.5 us -> 18.6 us
  between operations: 14.9 us -> 0.69 us
    pallas_call x0 -> x3, Pallas kernels: none -> 604 us  [call(): pl.pallas_call(kernel, out_shape=tuple((jax.ShapeDtypeStruct(shape, kind)...]
    psum x4 -> x0, waiting for transfers between devices: 382 us -> none  [the longest x1 363 us: per_device(): lax.psum(query_sum.astype(jnp.bfloat16), 'dp').astype(jnp.float32)]
    reduce_scatter x4 -> x0, waiting for transfers between devices: 189 us -> none  [the longest x2 136 us: project_in(): return lax.psum_scatter(partial_sum, 'row', scatter_dimension=1, tiled=True)]
    psum x6 -> x0, blocking collectives: 97.9 us -> none  [the longest x1 45.1 us: per_device(): lax.psum((query_gain_back, key_gain_back), ('dp', 'row', 'col'))]
    all_gather x3 -> x0, waiting for transfers between devices: 81.9 us -> none  [the longest x2 60.8 us: input_gradients(): piece = lax.all_gather(local, 'row', axis=1, tiled=True)]
    dot_general x18 -> x0, matrix products: 57.5 us -> none  [the longest x2 12.1 us: project_in(): partial_sum = jnp.dot(normed, merged, preferred_element_type=jnp.float32)]
    reshape x7 -> x1, local copies, waits for them, and re-layouts: 24 us -> 1.5 us  [per_device(): seg_col = segments.reshape(tokens, 1)]
    another operation x4 -> x0, local copies, waits for them, and re-layouts: 18.8 us -> none
  transfers between devices with their start and end apart: 11 -> 0, of which waited for: 9 -> 0; matrix products, arithmetic and copies ran while one was open for 12% -> 0% of each run, Pallas kernels for 0% -> 0%
where the time goes in v1:
time: 629 us
  Pallas kernels  604 us (96%)
  other arithmetic  18.6 us (3%)
    pallas_call x3, Pallas kernels, call(): pl.pallas_call(kernel, out_shape=tuple((jax.ShapeDtypeStruct(shape, kind)...  604 us
    convert_element_type x7, other arithmetic, per_device(): partial_sum.astype(wide)  18 us

profile of v1, /device:TPU:0, one launch (start us, length us, event | category | flops | bytes accessed | tf_op | source)
XLA Modules:
  0.0 629.2 jit_solution(12707310438097850922)
XLA Ops:
  0.6 1.5 copy.27.seg_col
  2.2 0.6 maximum_bitcast_fusion.inverse
  2.7 139.2 %shard_map.237 = (bf16[384,512]{1,0:T(8,128)(2,1)}, f32[384,128]{1,0:T(8,128)}, f32[384,384]{1,0:T(8,128)}, bf16[384,512]{1,0:T(8,128)(2,1)}, f32[2,384,384]{2,1...) custom-call(bf16[384,512]{1,0:T(8,128)(2,1)} %x.3, ...), custom_call_target="tpu_custom_call" | custom-call | tf_op jit(solution)/shard_map/pallas_call | solution.py:851
  142.0 152.9 %shard_map.238 = (bf16[384,512]{1,0:T(8,128)(2,1)}, f32[384,512]{1,0:T(8,128)}, f32[16,512]{1,0:T(8,128)}, bf16[512,1024]{1,0:T(8,128)(2,1)}, bf16[512,512]{1,0:...) custom-call(bf16[384,512]{1,0:T(8,128)(2,1)} %x.3, ...), custom_call_target="tpu_custom_call" | custom-call | tf_op jit(solution)/shard_map/pallas_call | solution.py:851
  294.9 311.9 %shard_map.239 = (f32[16,512]{1,0:T(8,128)}, bf16[512,1024]{1,0:T(8,128)(2,1)}, bf16[512,512]{1,0:T(8,128)(2,1)}, bf16[512,512]{1,0:T(8,128)(2,1)}, bf16[1024,51...) custom-call(f32[16,512]{1,0:T(8,128)} %get-tuple-element.57.refs_0_, ...), custom_call_target="tpu_custom_call" | custom-call | tf_op jit(solution)/shard_map/pallas_call | solution.py:851
  606.8 0.0 copy-start.1
  606.8 5.5 convert_element_type.25
  612.4 0.0 copy-done.1
  612.4 0.0 copy-start
  612.4 3.5 convert_element_type.26
  615.9 0.0 copy-done
  615.9 0.0 copy-start.3
  615.9 3.6 convert_element_type.27
  619.5 0.0 copy-start.2
  619.5 0.0 copy-done.3
  619.5 0.0 copy-start.6
  619.5 1.6 convert_element_type.21
  621.1 0.0 copy-start.5
  621.1 0.0 copy-done.2
  621.1 0.0 copy-start.7
  621.1 0.0 copy-start.4
  621.1 1.6 convert_element_type.24
  622.7 0.0 copy-done.6
  622.7 1.1 convert_element_type.22
  623.8 0.0 copy-done.5
  623.8 1.1 convert_element_type.23
  624.9 1.4 fusion
  626.3 1.3 slice_bitcast_fusion
  627.6 0.0 copy-done.7
  627.6 0.7 copy.30
  628.3 0.0 copy-done.4
  628.3 0.9 copy.31
  (1 shorter events, 0.0 us)
Async XLA Ops:
  606.8 5.6 copy-start.1
  612.4 3.5 copy-start
  615.9 3.6 copy-start.3
  619.5 1.6 copy-start.2
  619.5 3.2 copy-start.6
  621.1 2.7 copy-start.5
  621.1 6.5 %copy-start.7 = (bf16[384,512]{1,0:T(8,128)(2,1)S(1)}, bf16[384,512]{1,0:T(8,128)(2,1)}, u32[]{:S(2)}) copy-start(bf16[384,512]{1,0:T(8,128)(2,1)} %get-tuple-element.90) | copy-start | bytes 1179652
  621.1 7.2 %copy-start.4 = (f32[384,512]{1,0:T(8,128)S(1)}, f32[384,512]{1,0:T(8,128)}, u32[]{:S(2)}) copy-start(f32[384,512]{1,0:T(8,128)} %get-tuple-element.91) | copy-start | bytes 2359300

commit v2 on v1

--- a/solution.py
+++ b/solution.py
@@ -133,6 +133,7 @@
 def forward_kernel(
     rows_of,
     cols_of,
+    need,
     x,
     seg_row,
     seg_col,
@@ -240,6 +241,7 @@
         qkv.start(shift)
     project(me, pq_own, None)
 
+    need("wd", "ct")
     back = row_exchange(1, lambda shift: ph_s.at[shift - 1], ph_r)
     for shift in range(1, rows_of):
         ph_s[shift - 1] = dot_t(ct[...], wd[window(back.target(shift), fw), :]).astype(low)
@@ -304,6 +306,7 @@
     gather = row_exchange(2, lambda shift: mixed.at[0], mixed_r)
     for shift in range(1, rows_of):
         gather.start(shift)
+    need("wo")
     ox_s[...] = dot(mixed[0], wo[window(me, qw), :])
     for shift in range(1, rows_of):
         gather.arrive(shift)
@@ -332,6 +335,7 @@
     for shift in range(1, rows_of):
         stat2.start(shift)
 
+    need("wg", "wu")
     feed = row_exchange(3, lambda shift: pg_s.at[shift - 1], pg_r)
     for shift in range(1, rows_of):
         columns = window(feed.target(shift), fw)
@@ -376,9 +380,175 @@
         exchange.finish()
 
 
+def split(rows, columns):
+    count = 1
+    while rows % count or (rows // count) * columns > chunk_limit:
+        count += 1
+    return count
+
+
+class Line:
+    def __init__(self, members, out, near, far, spares, sems):
+        self.members, self.out, self.near, self.far = members, out, near, far
+        self.spares = spares
+        self.in_send, self.near_sem, self.far_sem, self.out_send, self.load_sem = sems
+        me = lax.axis_index("dp")
+        half = members // 2
+        left = me < half
+        place = jnp.where(left, half - 1 - me, me - half)
+        self.inner = jnp.where(left, me + 1, me - 1)
+        self.outer = jnp.where(left, jnp.maximum(me - 1, 0), jnp.minimum(me + 1, members - 1))
+        self.is_mid = place == 0
+        self.not_mid = place > 0
+        self.has_outer = place < half - 1
+        self.is_end = place == half - 1
+        self.chunks, self.done = [], 0
+
+    def view(self, refs, index):
+        which, row, rows, column, columns = self.chunks[index]
+        if not isinstance(row, int):
+            row = pl.multiple_of(row, 16)
+        if not isinstance(column, int):
+            column = pl.multiple_of(column, lanes)
+        return refs[which].at[pl.ds(row, rows), pl.ds(column, columns)]
+
+    def inward(self, index, target, sem):
+        return remote(
+            self.view(self.out, index),
+            self.view(target, index),
+            self.in_send.at[index],
+            sem.at[index],
+            "dp",
+            self.inner,
+        )
+
+    def outward(self, index):
+        return remote(
+            self.view(self.out, index),
+            self.view(self.far, index),
+            self.out_send.at[index],
+            self.far_sem.at[index],
+            "dp",
+            self.outer,
+        )
+
+    def send_in(self, index):
+        @pl.when(self.is_mid)
+        def _():
+            self.inward(index, self.far, self.far_sem).start()
+
+        @pl.when(self.not_mid)
+        def _():
+            self.inward(index, self.near, self.near_sem).start()
+
+    def release(self, which, row, rows, column, columns):
+        if self.members == 1:
+            return
+        count = split(rows, columns)
+        for part in range(count):
+            size = rows // count
+            self.chunks.append((which, row + part * size, size, column, columns))
+            index = len(self.chunks) - 1
+
+            @pl.when(self.is_end)
+            def _(index=index):
+                self.send_in(index)
+
+    def spare(self, index, kind):
+        _, _, rows, _, columns = self.chunks[index]
+        for ref in self.spares:
+            if ref.shape[1:] == (rows, columns):
+                return ref.at[kind]
+        raise ValueError("no spare")
+
+    def load(self, index, kind):
+        source = self.view((self.near, self.far)[kind], index)
+        return pltpu.make_async_copy(source, self.spare(index, kind), self.load_sem.at[kind])
+
+    def add(self, index, kind):
+        target, other = self.view(self.out, index), self.spare(index, kind)
+        rows = other.shape[0]
+        tile = 32 if rows % 32 == 0 else rows
+
+        def step(part, carry):
+            spot = pl.ds(pl.multiple_of(part * tile, 16), tile)
+            target[spot, :] = (target[spot, :].astype(wide) + other[spot, :].astype(wide)).astype(low)
+            return carry
+
+        lax.fori_loop(0, rows // tile, step, 0)
+
+    def begin_total(self, index):
+        @pl.when(self.is_mid)
+        def _():
+            self.inward(index, self.far, self.far_sem).wait_recv()
+            self.load(index, 1).start()
+
+    def end_total(self, index):
+        @pl.when(self.is_mid)
+        def _():
+            self.load(index, 1).wait()
+            self.inward(index, self.far, self.far_sem).wait_send()
+            self.add(index, 1)
+
+            @pl.when(self.has_outer)
+            def _():
+                self.outward(index).start()
+
+    def advance(self, count):
+        if self.members == 1:
+            return
+        for _ in range(count):
+            index = self.done
+            self.done += 1
+
+            @pl.when(self.has_outer)
+            def _():
+                self.inward(index, self.near, self.near_sem).wait_recv()
+                self.load(index, 0).start()
+
+            if index:
+                self.begin_total(index - 1)
+
+            @pl.when(self.has_outer)
+            def _():
+                self.load(index, 0).wait()
+                self.add(index, 0)
+                self.send_in(index)
+
+            if index:
+                self.end_total(index - 1)
+
+    def settle(self):
+        total = len(self.chunks)
+        self.advance(total - self.done)
+        self.begin_total(total - 1)
+        self.end_total(total - 1)
+
+        @pl.when(self.not_mid)
+        def _():
+            for index in range(total):
+                self.inward(index, self.far, self.far_sem).wait_recv()
+                self.inward(index, self.near, self.near_sem).wait_send()
+                source, target = self.view(self.far, index), self.view(self.out, index)
+                copy = pltpu.make_async_copy(source, target, self.load_sem.at[0])
+                copy.start()
+                copy.wait()
+
+                @pl.when(self.has_outer)
+                def _():
+                    self.outward(index).start()
+
+        @pl.when(self.has_outer)
+        def _():
+            for index in range(total):
+                self.outward(index).wait_send()
+
+
 def backward_kernel(
     rows_of,
     cols_of,
+    members,
+    need,
     x,
     ct,
     n1,
@@ -414,7 +584,11 @@
     gg,
     gu,
     gd,
-    hid_r,
+    *rest,
+):
+    near, far, rest = rest[:7], rest[7:14], rest[14:]
+    (
+        hid_r,
     gub_r,
     n_t,
     mb,
@@ -435,9 +609,18 @@
     row_recv,
     stat_send,
     stat_recv,
-    col_send,
-    col_recv,
-):
+        col_send,
+        col_recv,
+        small_r,
+        small_send,
+        small_recv,
+        in_send,
+        near_sem,
+        far_sem,
+        out_send,
+        load_sem,
+        *spares,
+    ) = rest
     tokens, depth = x.shape
     width = depth * rows_of
     qw, kw, fw = wq.shape[1] // rows_of, wk.shape[1] // rows_of, wg.shape[1] // rows_of
@@ -446,7 +629,15 @@
     group = heads // key_heads
     scale = size ** (-0.5)
     me = lax.axis_index("row")
-    greet((("row", rows_of), ("col", cols_of)))
+    greet((("row", rows_of), ("col", cols_of), ("dp", members)))
+    line = Line(
+        members,
+        (gq, gk, gv, go, gg, gu, gd),
+        near,
+        far,
+        spares,
+        (in_send, near_sem, far_sem, out_send, load_sem),
+    )
 
     def row_exchange(kind, send, receive):
         return Exchange("row", rows_of, send, receive, row_send.at[kind], row_recv.at[kind])
@@ -496,11 +687,14 @@
         else:
             ox_s[0, body, :] += part
         gd[index, :] = t_dot(piece, cut).astype(low)
+        line.release(6, hide.source(shift) * fw, fw, 0, depth)
     column0 = column_exchange(0)
     for shift in range(1, cols_of):
         column0.start(shift)
     n_t[...] = n2[...].T
+    need("wg", "wu")
     for shift in range(rows_of):
+        line.advance(1)
         if shift:
             gates.arrive(shift)
         piece = gub if shift == 0 else gub_r.at[shift - 1]
@@ -510,6 +704,10 @@
             ox_s[1, body, :] = part
         else:
             ox_s[1, body, :] += part
+        gg[:, index] = dot(n_t[...], piece[:, :fw]).astype(low)
+        line.release(4, 0, depth, gates.source(shift) * fw, fw)
+        gu[:, index] = dot(n_t[...], piece[:, fw:]).astype(low)
+        line.release(5, 0, depth, gates.source(shift) * fw, fw)
     column1 = column_exchange(1)
     for shift in range(1, cols_of):
         column1.start(shift)
@@ -541,10 +739,7 @@
     stat_s[0, pad] = jnp.zeros((8, lanes), wide)
     for shift in range(1, rows_of):
         stat2.start(shift)
-    for shift in range(rows_of):
-        piece = gub if shift == 0 else gub_r.at[shift - 1]
-        index = window(gates.source(shift), fw)
-        gg[:, index] = dot(n_t[...], piece[:, :fw]).astype(low)
+    need("wo", "mixed", "lows", "shares")
     for shift in range(1, rows_of):
         stat2.arrive(shift)
 
@@ -567,6 +762,8 @@
     for shift in range(rows_of):
         index = window(blend.source(shift), qw)
         go[index, :] = t_dot(mixed[shift], ml[...]).astype(low)
+        line.release(3, blend.source(shift) * qw, qw, 0, depth)
+    line.advance(2)
     for shift in range(1, rows_of):
         blend.arrive(shift)
 
@@ -588,6 +785,7 @@
 
     blend.finish()
     each_tile(tokens, share_back)
+    need("n1", "raw", "trig")
     n_t[...] = n1[...].T
 
     def pull(head, back, gain, row):
@@ -617,6 +815,8 @@
     deliver = row_exchange(3, lambda shift: dqkv, dqkv_r)
     for shift in range(1, rows_of):
         deliver.start(shift)
+    need("wq", "wk", "wv")
+    line.advance(1)
     for shift in range(rows_of):
         if shift:
             deliver.arrive(shift)
@@ -640,8 +840,12 @@
         gq[:, window(source, qw)] = dot(n_t[...], piece[:, :qw]).astype(low)
         gk[:, window(source, kw)] = dot(n_t[...], piece[:, qw : qw + kw]).astype(low)
         gv[:, window(source, kw)] = dot(n_t[...], piece[:, qw + kw :]).astype(low)
+    line.release(0, 0, depth, 0, qw * rows_of)
+    line.release(1, 0, depth, 0, kw * rows_of)
+    line.release(2, 0, depth, 0, kw * rows_of)
     for shift in range(1, cols_of):
         column2.arrive(shift)
+    need("x", "fs")
 
     stat1 = stat_exchange(1)
 
@@ -660,11 +864,6 @@
     stat_r[1, me, pad] = summed
     for shift in range(1, rows_of):
         stat1.start(shift)
-    n_t[...] = n2[...].T
-    for shift in range(rows_of):
-        piece = gub if shift == 0 else gub_r.at[shift - 1]
-        index = window(gates.source(shift), fw)
-        gu[:, index] = dot(n_t[...], piece[:, fw:]).astype(low)
     for shift in range(1, rows_of):
         stat1.arrive(shift)
 
@@ -676,188 +875,67 @@
 
     each_tile(tokens, finish)
     small[8:16, :lanes] = stat1.total(pad)
+    ranked = Ranked("dp", members, lambda shift: small, small_r, small_send, small_recv)
+    if members > 1:
+        small_r[lax.axis_index("dp")] = small[...]
+        for shift in range(1, members):
+            ranked.start(shift)
+        line.settle()
+        for shift in range(1, members):
+            ranked.arrive(shift)
+        ranked.finish()
+        summed = small_r[0]
+        for member in range(1, members):
+            summed = summed + small_r[member]
+        small[...] = summed
     for exchange in (hide, gates, column0, column1, stat2, deliver, column2, stat1):
         exchange.finish()
 
 
-def chunks_of(shape):
-    rows, columns = shape
-    count = 1
-    while rows % count or (rows // count) * columns > chunk_limit:
-        count += 1
-    return count, rows // count
-
-
-def combine_kernel(members, shapes, *refs):
-    count = len(shapes)
-    small, *own = refs[: count + 1]
-    small_out, *out = refs[count + 1 : 2 * count + 2]
-    near = refs[2 * count + 2 : 3 * count + 2]
-    far = refs[3 * count + 2 : 4 * count + 2]
-    small_r, in_send, near_sem, far_sem, out_send, small_send, small_recv = refs[4 * count + 2 :]
-    greet((("dp", members),))
-    me = lax.axis_index("dp")
-    half = members // 2
-    left = me < half
-    place = jnp.where(left, half - 1 - me, me - half)
-    inner = jnp.where(left, me + 1, me - 1)
-    outer = jnp.where(left, jnp.maximum(me - 1, 0), jnp.minimum(me + 1, members - 1))
-    is_mid = place == 0
-    has_outer = place < half - 1
-    ranked = Ranked("dp", members, lambda shift: small, small_r, small_send, small_recv)
-    small_r[me] = small[...]
-    for shift in range(1, members):
-        ranked.start(shift)
-
-    bases, base = [], 0
-    for shape in shapes:
-        bases.append(base)
-        base += chunks_of(shape)[0]
-
-    def inward(which, index, source, target, target_sem):
-        rows = chunks_of(shapes[which])[1]
-        spot = pl.ds(pl.multiple_of(index * rows, 16), rows)
-        slot = bases[which] + index
-        return remote(
-            source[which].at[spot],
-            target[which].at[spot],
-            in_send.at[slot],
-            target_sem.at[slot],
-            "dp",
-            inner,
-        )
-
-    def outward(which, index):
-        rows = chunks_of(shapes[which])[1]
-        spot = pl.ds(pl.multiple_of(index * rows, 16), rows)
-        slot = bases[which] + index
-        return remote(
-            out[which].at[spot],
-            far[which].at[spot],
-            out_send.at[slot],
-            far_sem.at[slot],
-            "dp",
-            outer,
-        )
-
-    def add(which, index, first, second, target):
-        rows = chunks_of(shapes[which])[1]
-        spot = pl.ds(pl.multiple_of(index * rows, 16), rows)
-        total = first[which][spot, :].astype(wide) + second[which][spot, :].astype(wide)
-        target[which][spot, :] = total.astype(low)
-
-    def send_in(which, index):
-        target, sem = near, near_sem
-
-        @pl.when(has_outer)
-        def _():
-            inward(which, index, near, near, near_sem).wait_recv()
-            add(which, index, own, near, near)
-
-            @pl.when(is_mid)
-            def _():
-                inward(which, index, near, far, far_sem).start()
-
-            @pl.when(jnp.logical_not(is_mid))
-            def _():
-                inward(which, index, near, near, near_sem).start()
-
-        @pl.when(jnp.logical_not(has_outer))
-        def _():
-            @pl.when(is_mid)
-            def _():
-                inward(which, index, own, far, far_sem).start()
-
-            @pl.when(jnp.logical_not(is_mid))
-            def _():
-                inward(which, index, own, near, near_sem).start()
-
-    def finish_chunk(which, index):
-        inward(which, index, own, far, far_sem).wait_recv()
-
-        @pl.when(is_mid)
-        def _():
-            @pl.when(has_outer)
-            def _():
-                add(which, index, near, far, out)
-
-            @pl.when(jnp.logical_not(has_outer))
-            def _():
-                add(which, index, own, far, out)
-
-        @pl.when(jnp.logical_not(is_mid))
-        def _():
-            rows = chunks_of(shapes[which])[1]
-            spot = pl.ds(pl.multiple_of(index * rows, 16), rows)
-            out[which][spot, :] = far[which][spot, :]
-
-        @pl.when(has_outer)
-        def _():
-            outward(which, index).start()
-
-    def over(which, body):
-        def step(index, carry):
-            body(index)
-            return carry
-
-        lax.fori_loop(0, chunks_of(shapes[which])[0], step, 0)
-
-    @pl.when(is_mid)
-    def _():
-        for which in range(count):
-
-            def both(index, which=which):
-                send_in(which, index)
-
-                @pl.when(index > 0)
-                def _():
-                    finish_chunk(which, index - 1)
-
-            over(which, both)
-            finish_chunk(which, chunks_of(shapes[which])[0] - 1)
-
-    @pl.when(jnp.logical_not(is_mid))
-    def _():
-        for which in range(count):
-            over(which, lambda index, which=which: send_in(which, index))
-        for which in range(count):
-            over(which, lambda index, which=which: finish_chunk(which, index))
-
-    for shift in range(1, members):
-        ranked.arrive(shift)
-    result = small_r[0]
-    for member in range(1, members):
-        result = result + small_r[member]
-    small_out[...] = result
-    ranked.finish()
-    for which in range(count):
-
-        def drain(index, which=which):
-            inward(which, index, own, near, near_sem).wait_send()
-
-            @pl.when(has_outer)
-            def _():
-                outward(which, index).wait_send()
-
-        over(which, drain)
-
-
 def vmem(shape, kind):
     return pltpu.VMEM(shape, kind)
 
 
-def call(kernel, shapes, scratch, identity, arguments):
-    inside = pl.BlockSpec(memory_space=pltpu.VMEM)
+def call(kernel, shapes, scratch, identity, arguments, late=(), outside=()):
+    inside, away = pl.BlockSpec(memory_space=pltpu.VMEM), pl.BlockSpec(memory_space=pl.ANY)
+    names = list(arguments)
+    late = [name for name in names if name in late]
+
+    def body(*refs):
+        given = dict(zip(names, refs))
+        rest = refs[len(names) :]
+        copies = {}
+        if late:
+            holders, sem = rest[-len(late) - 1 : -1], rest[-1]
+            rest = rest[: -len(late) - 1]
+            for index, name in enumerate(late):
+                copies[name] = pltpu.make_async_copy(given[name], holders[index], sem.at[index])
+                copies[name].start()
+                given[name] = holders[index]
+
+        def need(*wanted):
+            for name in wanted:
+                copy = copies.pop(name, None)
+                if copy is not None:
+                    copy.wait()
+
+        kernel(need, *given.values(), *rest)
+        need(*list(copies))
+
+    extra = []
+    if late:
+        extra = [vmem(arguments[name].shape, arguments[name].dtype) for name in late]
+        extra.append(pltpu.SemaphoreType.DMA((len(late),)))
     return pl.pallas_call(
-        kernel,
+        body,
         out_shape=tuple(jax.ShapeDtypeStruct(shape, kind) for shape, kind in shapes),
-        in_specs=[inside] * len(arguments),
-        out_specs=tuple([inside] * len(shapes)),
-        scratch_shapes=scratch,
+        in_specs=[away if name in late else inside for name in names],
+        out_specs=tuple(away if index in outside else inside for index in range(len(shapes))),
+        scratch_shapes=scratch + extra,
         compiler_params=pltpu.CompilerParams(
             collective_id=identity, has_side_effects=True, vmem_limit_bytes=full_vmem
         ),
-    )(*arguments)
+    )(*arguments.values())
 
 
 def per_device(
@@ -939,34 +1017,48 @@
         ]
         + sems(1),
         0,
-        (
-            block_input,
-            seg_row,
-            seg_col,
-            inverse,
-            gain1,
-            query_weight,
-            key_weight,
-            value_weight,
-            qn,
-            kn,
-            output_weight,
-            gain2,
-            gate_weight,
-            up_weight,
-            down_weight,
-            cotangent,
+        dict(
+            x=block_input,
+            seg_row=seg_row,
+            seg_col=seg_col,
+            inverse=inverse,
+            gain1=gain1,
+            wq=query_weight,
+            wk=key_weight,
+            wv=value_weight,
+            qn=qn,
+            kn=kn,
+            wo=output_weight,
+            gain2=gain2,
+            wg=gate_weight,
+            wu=up_weight,
+            wd=down_weight,
+            ct=cotangent,
         ),
+        late=("wo", "wg", "wu", "wd", "ct"),
+    )
+    saved = dict(
+        zip(("n1", "fs", "raw", "lows", "shares", "trig", "mixed", "mid", "ss", "n2", "hid", "gub"), saved)
     )
     weights = (query_weight, key_weight, value_weight, output_weight, gate_weight, up_weight)
     shapes = [weight.shape for weight in weights] + [down_weight.shape]
-    block_output, input_gradient, small, *partials = call(
-        partial(backward_kernel, rows_of, cols_of),
+    pieces = {
+        (fw, depth): rows_of,
+        (depth, fw): 2 * rows_of,
+        (qw, depth): rows_of,
+        (depth, qw * rows_of): 1,
+        (depth, kw * rows_of): 2,
+    }
+    slots = sum(split(*shape) * times for shape, times in pieces.items())
+    spares = {(shape[0] // split(*shape), shape[1]) for shape in pieces}
+    peers = max(members - 1, 1)
+    done = call(
+        partial(backward_kernel, rows_of, cols_of, members),
         (
             ((tokens, depth), low),
             ((tokens, depth), wide),
             ((16, depth), wide),
-            *((shape, low) for shape in shapes),
+            *((shape, low) for shape in shapes * 3),
         ),
         [
             vmem((others, tokens, fw), low),
@@ -987,32 +1079,32 @@
             vmem((3, tokens + 8, depth), wide),
             vmem((3, beside, tokens + 8, depth), wide),
         ]
-        + sems(3),
+        + sems(3)
+        + [vmem((members, 16, depth), wide), dma((peers,)), dma((peers,))]
+        + [dma((slots,))] * 4
+        + [dma((2,))]
+        + [vmem((2, *shape), low) for shape in sorted(spares)],
         1,
-        (
-            block_input,
-            cotangent,
-            *saved,
-            gain1,
-            gain2,
-            qn,
-            kn,
-            *weights,
-            down_weight,
+        dict(
+            x=block_input,
+            ct=cotangent,
+            **saved,
+            gain1=gain1,
+            gain2=gain2,
+            qn=qn,
+            kn=kn,
+            wq=query_weight,
+            wk=key_weight,
+            wv=value_weight,
+            wo=output_weight,
+            wg=gate_weight,
+            wu=up_weight,
+            wd=down_weight,
         ),
+        late=("x", "n1", "fs", "raw", "lows", "shares", "trig", "mixed", "wq", "wk", "wv", "wo", "wg", "wu"),
+        outside=range(10, 24),
     )
-    if members > 1:
-        slots = sum(chunks_of(shape)[0] for shape in shapes)
-        small, *partials = call(
-            partial(combine_kernel, members, shapes),
-            (((16, depth), wide), *((shape, low) for shape in shapes)),
-            [vmem(shape, low) for shape in shapes] * 2
-            + [vmem((members, 16, depth), wide)]
-            + [dma((slots,))] * 4
-            + [dma((members - 1,))] * 2,
-            2,
-            (small, *partials),
-        )
+    block_output, input_gradient, small, *partials = done[:10]
     gq, gk, gv, go, gg, gu, gd = (partial_sum.astype(wide) for partial_sum in partials)
     return (
         block_output,

time: 629 us -> 575 us (0.914)
  Pallas kernels: 604 us -> 548 us
    pallas_call x3 -> x2, Pallas kernels: 604 us -> 548 us  [call(): pl.pallas_call(body, out_shape=tuple((jax.ShapeDtypeStruct(shape, kind) f...]
where the time goes in v2:
time: 575 us; the launch traced here: 574 us
  Pallas kernels  548 us (95%)
  other arithmetic  18.8 us (3%)
  local copies, waits for them, and re-layouts  5.81 us (1%)
    pallas_call x2, Pallas kernels, call(): pl.pallas_call(body, out_shape=tuple((jax.ShapeDtypeStruct(shape, kind) f...  548 us
    convert_element_type x7, other arithmetic, per_device(): partial_sum.astype(wide)  18.2 us

profile of v2, /device:TPU:0, one launch (start us, length us, event | category | flops | bytes accessed | tf_op | source)
XLA Modules:
  0.0 573.6 jit_solution(16045595861273558283)
XLA Ops:
  0.7 0.6 maximum_bitcast_fusion.refs_3_
  1.2 1.5 copy.27.refs_2_
  2.7 136.1 %shard_map.237 = (bf16[384,512]{1,0:T(8,128)(2,1)}, f32[384,128]{1,0:T(8,128)}, f32[384,384]{1,0:T(8,128)}, bf16[384,512]{1,0:T(8,128)(2,1)}, f32[2,384,384]{2,1...) custom-call(bf16[384,512]{1,0:T(8,128)(2,1)} %refs_0_.3, ...), custom_call_target="tpu_custom_call" | custom-call | tf_op jit(solution)/shard_map/pallas_call | solution.py:929
  138.9 412.3 %shard_map.238 = (bf16[384,512]{1,0:T(8,128)(2,1)}, f32[384,512]{1,0:T(8,128)}, f32[16,512]{1,0:T(8,128)}, bf16[512,1024]{1,0:T(8,128)(2,1)}, bf16[512,512]{1,0:...) custom-call(bf16[384,512]{1,0:T(8,128)(2,1)} %refs_0_.3, ...), custom_call_target="tpu_custom_call" | custom-call | tf_op jit(solution)/shard_map/pallas_call | solution.py:929
  551.1 0.0 copy-start.4
  551.1 1.3 slice_bitcast_fusion
  552.4 1.4 fusion
  553.8 0.0 copy-start.3
  553.8 2.2 convert_element_type.22
  556.0 2.1 convert_element_type.23
  558.2 0.0 copy-done.4
  558.2 0.0 copy-start.2
  558.2 1.6 convert_element_type.21
  559.8 0.0 copy-done.3
  559.8 1.6 convert_element_type.24
  561.4 0.0 copy-done.2
  561.4 0.0 copy-start.1
  561.4 3.5 convert_element_type.25
  564.9 0.0 copy-done.1
  564.9 0.0 copy-start
  564.9 3.5 convert_element_type.26
  568.4 0.0 copy-done
  568.4 0.0 copy-start.6
  568.4 0.0 copy-start.5
  568.4 3.6 convert_element_type.27
  572.0 0.0 copy-done.6
  572.0 0.7 copy.30
  572.7 0.0 copy-done.5
  572.8 0.9 copy.31
  (1 shorter events, 0.0 us)
Async XLA Ops:
  551.1 7.1 %copy-start.4 = (bf16[512,1024]{1,0:T(8,128)(2,1)S(1)}, bf16[512,1024]{1,0:T(8,128)(2,1)}, u32[]{:S(2)}) copy-start(bf16[512,1024]{1,0:T(8,128)(2,1)} %get-tuple-element.50) | copy-start | bytes 3145732
  553.8 6.0 %copy-start.3 = (bf16[1024,512]{1,0:T(8,128)(2,1)S(1)}, bf16[1024,512]{1,0:T(8,128)(2,1)}, u32[]{:S(2)}) copy-start(bf16[1024,512]{1,0:T(8,128)(2,1)} %get-tuple-element.53) | copy-start | bytes 3145732
  558.2 3.2 copy-start.2
  561.4 3.5 copy-start.1
  564.9 3.5 copy-start
  568.4 3.6 copy-start.6
  568.4 4.4 copy-start.5

commit v3 on v2

--- a/solution.py
+++ b/solution.py
@@ -12,6 +12,7 @@
 lanes = 128
 full_vmem = 67043328
 chunk_limit = 262144
+lag = 2
 low = jnp.bfloat16
 wide = jnp.float32
 
@@ -148,8 +149,6 @@
     gain2,
     wg,
     wu,
-    wd,
-    ct,
     n1,
     fs,
     raw,
@@ -161,14 +160,11 @@
     ss,
     n2,
     hid,
-    gub,
+    slope,
     unit,
     pq_own,
     pq_s,
     pq_r,
-    ph_own,
-    ph_s,
-    ph_r,
     pg_own,
     pg_s,
     pg_r,
@@ -241,13 +237,6 @@
         qkv.start(shift)
     project(me, pq_own, None)
 
-    need("wd", "ct")
-    back = row_exchange(1, lambda shift: ph_s.at[shift - 1], ph_r)
-    for shift in range(1, rows_of):
-        ph_s[shift - 1] = dot_t(ct[...], wd[window(back.target(shift), fw), :]).astype(low)
-        back.start(shift)
-    ph_own[...] = dot_t(ct[...], wd[window(me, fw), :])
-
     def tables(rows, start, tile):
         key = lax.broadcasted_iota(jnp.int32, (tile, tokens), 1)
         query = lax.broadcasted_iota(jnp.int32, (tile, tokens), 0) + start
@@ -346,7 +335,6 @@
     pg_own[:, fw:] = dot(unit[...], wu[:, window(me, fw)])
     for shift in range(1, rows_of):
         stat2.arrive(shift)
-        back.arrive(shift)
 
     def scale_rows(rows, start, tile):
         second = lax.rsqrt(stat2.total(rows) / width + epsilon)
@@ -366,17 +354,14 @@
             upward = upward + pg_r[shift - 1, rows, fw:].astype(wide)
         gate = gate * second
         upward = upward * second
-        behind = ph_own[rows, :]
-        for shift in range(1, rows_of):
-            behind = behind + ph_r[shift - 1, rows, :].astype(wide)
         sigmoid = jax.nn.sigmoid(gate)
         silu = gate * sigmoid
         hid[rows, :] = (silu * upward).astype(low)
-        gub[rows, :fw] = (behind * upward * sigmoid * (1.0 + gate * (1.0 - sigmoid))).astype(low)
-        gub[rows, fw:] = (behind * silu).astype(low)
+        slope[rows, :fw] = upward * sigmoid * (1.0 + gate * (1.0 - sigmoid))
+        slope[rows, fw:] = silu
 
     each_tile(tokens, activate)
-    for exchange in (stat1, qkv, back, gather, column, stat2, feed):
+    for exchange in (stat1, qkv, gather, column, stat2, feed):
         exchange.finish()
 
 
@@ -391,7 +376,7 @@
     def __init__(self, members, out, near, far, spares, sems):
         self.members, self.out, self.near, self.far = members, out, near, far
         self.spares = spares
-        self.in_send, self.near_sem, self.far_sem, self.out_send, self.load_sem = sems
+        self.in_send, self.near_sem, self.far_sem, self.out_send, self.store_sem, self.load_sem = sems
         me = lax.axis_index("dp")
         half = members // 2
         left = me < half
@@ -432,6 +417,16 @@
             self.outer,
         )
 
+    def relay(self, index):
+        return remote(
+            self.view(self.far, index),
+            self.view(self.far, index),
+            self.out_send.at[index],
+            self.far_sem.at[index],
+            "dp",
+            self.outer,
+        )
+
     def send_in(self, index):
         @pl.when(self.is_mid)
         def _():
@@ -483,6 +478,11 @@
             self.inward(index, self.far, self.far_sem).wait_recv()
             self.load(index, 1).start()
 
+    def store(self, index):
+        return pltpu.make_async_copy(
+            self.view(self.out, index), self.view(self.far, index), self.store_sem.at[index]
+        )
+
     def end_total(self, index):
         @pl.when(self.is_mid)
         def _():
@@ -494,6 +494,8 @@
             def _():
                 self.outward(index).start()
 
+            self.store(index).start()
+
     def advance(self, count):
         if self.members == 1:
             return
@@ -506,8 +508,8 @@
                 self.inward(index, self.near, self.near_sem).wait_recv()
                 self.load(index, 0).start()
 
-            if index:
-                self.begin_total(index - 1)
+            if index >= lag:
+                self.begin_total(index - lag)
 
             @pl.when(self.has_outer)
             def _():
@@ -515,33 +517,40 @@
                 self.add(index, 0)
                 self.send_in(index)
 
-            if index:
-                self.end_total(index - 1)
+            if index >= lag:
+                self.end_total(index - lag)
 
     def settle(self):
         total = len(self.chunks)
         self.advance(total - self.done)
-        self.begin_total(total - 1)
-        self.end_total(total - 1)
+        for index in range(max(total - lag, 0), total):
+            self.begin_total(index)
+            self.end_total(index)
 
         @pl.when(self.not_mid)
         def _():
             for index in range(total):
                 self.inward(index, self.far, self.far_sem).wait_recv()
-                self.inward(index, self.near, self.near_sem).wait_send()
-                source, target = self.view(self.far, index), self.view(self.out, index)
-                copy = pltpu.make_async_copy(source, target, self.load_sem.at[0])
-                copy.start()
-                copy.wait()
 
                 @pl.when(self.has_outer)
                 def _():
-                    self.outward(index).start()
-
-        @pl.when(self.has_outer)
+                    self.relay(index).start()
+
+            for index in range(total):
+                self.inward(index, self.near, self.near_sem).wait_send()
+
+                @pl.when(self.has_outer)
+                def _():
+                    self.relay(index).wait_send()
+
+        @pl.when(self.is_mid)
         def _():
             for index in range(total):
-                self.outward(index).wait_send()
+                self.store(index).wait()
+
+                @pl.when(self.has_outer)
+                def _():
+                    self.outward(index).wait_send()
 
 
 def backward_kernel(
@@ -562,7 +571,7 @@
     ss,
     n2,
     hid,
-    gub,
+    slope,
     gain1,
     gain2,
     qn,
@@ -577,17 +586,15 @@
     bo,
     ig,
     small,
-    gq,
-    gk,
-    gv,
-    go,
-    gg,
-    gu,
-    gd,
     *rest,
 ):
-    near, far, rest = rest[:7], rest[7:14], rest[14:]
+    far, near, rest = rest[:7], rest[7:14], rest[14:]
+    grads, rest = rest[:7], rest[7:]
+    gq, gk, gv, go, gg, gu, gd = grads
     (
+        gub,
+        ph_s,
+        ph_r,
         hid_r,
     gub_r,
     n_t,
@@ -618,6 +625,7 @@
         near_sem,
         far_sem,
         out_send,
+        store_sem,
         load_sem,
         *spares,
     ) = rest
@@ -632,11 +640,11 @@
     greet((("row", rows_of), ("col", cols_of), ("dp", members)))
     line = Line(
         members,
-        (gq, gk, gv, go, gg, gu, gd),
+        grads,
         near,
         far,
         spares,
-        (in_send, near_sem, far_sem, out_send, load_sem),
+        (in_send, near_sem, far_sem, out_send, store_sem, load_sem),
     )
 
     def row_exchange(kind, send, receive):
@@ -672,10 +680,9 @@
     gates = row_exchange(1, lambda shift: gub, gub_r)
     for shift in range(1, rows_of):
         hide.start(shift)
-    for shift in range(1, rows_of):
-        gates.start(shift)
     body = pl.ds(0, tokens)
     cut = ct[...]
+    back = row_exchange(4, lambda shift: ph_s.at[shift - 1], ph_r)
     for shift in range(rows_of):
         if shift:
             hide.arrive(shift)
@@ -688,14 +695,35 @@
             ox_s[0, body, :] += part
         gd[index, :] = t_dot(piece, cut).astype(low)
         line.release(6, hide.source(shift) * fw, fw, 0, depth)
+        if shift == 0:
+            for other in range(1, rows_of):
+                ph_s[other - 1] = dot_t(cut, wd[window(back.target(other), fw), :]).astype(low)
+                back.start(other)
+        else:
+            line.advance(1)
     column0 = column_exchange(0)
     for shift in range(1, cols_of):
         column0.start(shift)
     n_t[...] = n2[...].T
+    need("slope")
+    line.advance(2)
+    for shift in range(1, rows_of):
+        back.arrive(shift)
+
+    def behind(rows, start, tile):
+        value = dot_t(ct[rows, :], wd[window(me, fw), :])
+        for shift in range(1, rows_of):
+            value = value + ph_r[shift - 1, rows, :].astype(wide)
+        gub[rows, :fw] = (value * slope[rows, :fw]).astype(low)
+        gub[rows, fw:] = (value * slope[rows, fw:]).astype(low)
+
+    each_tile(tokens, behind)
+    for shift in range(1, rows_of):
+        gates.start(shift)
     need("wg", "wu")
     for shift in range(rows_of):
-        line.advance(1)
         if shift:
+            line.advance(2)
             gates.arrive(shift)
         piece = gub if shift == 0 else gub_r.at[shift - 1]
         index = window(gates.source(shift), fw)
@@ -711,6 +739,7 @@
     column1 = column_exchange(1)
     for shift in range(1, cols_of):
         column1.start(shift)
+    line.advance(1)
     for shift in range(1, cols_of):
         column0.arrive(shift)
 
@@ -740,6 +769,7 @@
     for shift in range(1, rows_of):
         stat2.start(shift)
     need("wo", "mixed", "lows", "shares")
+    line.advance(1)
     for shift in range(1, rows_of):
         stat2.arrive(shift)
 
@@ -787,6 +817,7 @@
     each_tile(tokens, share_back)
     need("n1", "raw", "trig")
     n_t[...] = n1[...].T
+    line.advance(1)
 
     def pull(head, back, gain, row):
         raw_piece = raw[:, head * size : (head + 1) * size]
@@ -816,9 +847,9 @@
     for shift in range(1, rows_of):
         deliver.start(shift)
     need("wq", "wk", "wv")
-    line.advance(1)
     for shift in range(rows_of):
         if shift:
+            line.advance(1)
             deliver.arrive(shift)
         piece = dqkv if shift == 0 else dqkv_r.at[shift - 1]
         source = deliver.source(shift)
@@ -843,6 +874,7 @@
     line.release(0, 0, depth, 0, qw * rows_of)
     line.release(1, 0, depth, 0, kw * rows_of)
     line.release(2, 0, depth, 0, kw * rows_of)
+    line.advance(1)
     for shift in range(1, cols_of):
         column2.arrive(shift)
     need("x", "fs")
@@ -864,6 +896,7 @@
     stat_r[1, me, pad] = summed
     for shift in range(1, rows_of):
         stat1.start(shift)
+    line.advance(1)
     for shift in range(1, rows_of):
         stat1.arrive(shift)
 
@@ -888,7 +921,7 @@
         for member in range(1, members):
             summed = summed + small_r[member]
         small[...] = summed
-    for exchange in (hide, gates, column0, column1, stat2, deliver, column2, stat1):
+    for exchange in (hide, back, gates, column0, column1, stat2, deliver, column2, stat1):
         exchange.finish()
 
 
@@ -974,8 +1007,8 @@
 
     def sems(kinds):
         return [
-            dma((4, others)),
-            dma((4, others)),
+            dma((5, others)),
+            dma((5, others)),
             dma((2, others)),
             dma((2, others)),
             dma((kinds, beside)) if kinds > 1 else dma((beside,)),
@@ -996,16 +1029,13 @@
             ((tokens, lanes), wide),
             ((tokens, depth), low),
             ((tokens, fw), low),
-            ((tokens, 2 * fw), low),
+            ((tokens, 2 * fw), wide),
         ),
         [
             vmem((tokens, depth), low),
             vmem((tokens, total), wide),
             vmem((others, tokens, total), low),
             vmem((others, tokens, total), low),
-            vmem((tokens, fw), wide),
-            vmem((others, tokens, fw), low),
-            vmem((others, tokens, fw), low),
             vmem((tokens, 2 * fw), wide),
             vmem((others, tokens, 2 * fw), low),
             vmem((others, tokens, 2 * fw), low),
@@ -1032,13 +1062,11 @@
             gain2=gain2,
             wg=gate_weight,
             wu=up_weight,
-            wd=down_weight,
-            ct=cotangent,
         ),
-        late=("wo", "wg", "wu", "wd", "ct"),
+        late=("wo", "wg", "wu"),
     )
     saved = dict(
-        zip(("n1", "fs", "raw", "lows", "shares", "trig", "mixed", "mid", "ss", "n2", "hid", "gub"), saved)
+        zip(("n1", "fs", "raw", "lows", "shares", "trig", "mixed", "mid", "ss", "n2", "hid", "slope"), saved)
     )
     weights = (query_weight, key_weight, value_weight, output_weight, gate_weight, up_weight)
     shapes = [weight.shape for weight in weights] + [down_weight.shape]
@@ -1058,9 +1086,13 @@
             ((tokens, depth), low),
             ((tokens, depth), wide),
             ((16, depth), wide),
-            *((shape, low) for shape in shapes * 3),
+            *((shape, low) for shape in shapes * 2),
         ),
-        [
+        [vmem(shape, low) for shape in shapes]
+        + [
+            vmem((tokens, 2 * fw), low),
+            vmem((others, tokens, fw), low),
+            vmem((others, tokens, fw), low),
             vmem((others, tokens, fw), low),
             vmem((others, tokens, 2 * fw), low),
             vmem((depth, tokens), low),
@@ -1081,7 +1113,7 @@
         ]
         + sems(3)
         + [vmem((members, 16, depth), wide), dma((peers,)), dma((peers,))]
-        + [dma((slots,))] * 4
+        + [dma((slots,))] * 5
         + [dma((2,))]
         + [vmem((2, *shape), low) for shape in sorted(spares)],
         1,
@@ -1101,8 +1133,8 @@
             wu=up_weight,
             wd=down_weight,
         ),
-        late=("x", "n1", "fs", "raw", "lows", "shares", "trig", "mixed", "wq", "wk", "wv", "wo", "wg", "wu"),
-        outside=range(10, 24),
+        late=("x", "n1", "fs", "raw", "lows", "shares", "trig", "mixed", "slope", "wq", "wk", "wv", "wo", "wg", "wu"),
+        outside=range(3, 17),
     )
     block_output, input_gradient, small, *partials = done[:10]
     gq, gk, gv, go, gg, gu, gd = (partial_sum.astype(wide) for partial_sum in partials)

time: 575 us -> 476 us (0.83)
  Pallas kernels: 548 us -> 449 us
    pallas_call x2, Pallas kernels: 548 us -> 449 us  [call(): pl.pallas_call(body, out_shape=tuple((jax.ShapeDtypeStruct(shape, kind) f...]
where the time goes in v3:
time: 476 us; the launch traced here: 474 us
  Pallas kernels  449 us (94%)
  other arithmetic  18.8 us (4%)
  local copies, waits for them, and re-layouts  5.82 us (1%)
    pallas_call x2, Pallas kernels, call(): pl.pallas_call(body, out_shape=tuple((jax.ShapeDtypeStruct(shape, kind) f...  449 us
    convert_element_type x7, other arithmetic, per_device(): partial_sum.astype(wide)  18.2 us

profile of v3, /device:TPU:0, one launch (start us, length us, event | category | flops | bytes accessed | tf_op | source)
XLA Modules:
  0.0 474.1 jit_solution(7117077599068021597)
XLA Ops:
  0.7 0.6 maximum_bitcast_fusion.refs_3_
  1.2 1.5 copy.27.refs_2_
  2.7 115.0 %shard_map.237 = (bf16[384,512]{1,0:T(8,128)(2,1)}, f32[384,128]{1,0:T(8,128)}, f32[384,384]{1,0:T(8,128)}, bf16[384,512]{1,0:T(8,128)(2,1)}, f32[2,384,384]{2,1...) custom-call(bf16[384,512]{1,0:T(8,128)(2,1)} %refs_0_.3, ...), custom_call_target="tpu_custom_call" | custom-call | tf_op jit(solution)/shard_map/pallas_call | solution.py:962
  117.7 333.8 %shard_map.238 = (bf16[384,512]{1,0:T(8,128)(2,1)}, f32[384,512]{1,0:T(8,128)}, f32[16,512]{1,0:T(8,128)}, bf16[512,1024]{1,0:T(8,128)(2,1)}, bf16[512,512]{1,0:...) custom-call(bf16[384,512]{1,0:T(8,128)(2,1)} %refs_0_.3, ...), custom_call_target="tpu_custom_call" | custom-call | tf_op jit(solution)/shard_map/pallas_call | solution.py:962
  451.6 0.0 copy-start.4
  451.6 1.3 slice_bitcast_fusion
  452.9 1.4 fusion
  454.2 0.0 copy-start.3
  454.2 2.2 convert_element_type.22
  456.5 2.1 convert_element_type.23
  458.6 0.0 copy-done.4
  458.6 0.0 copy-start.2
  458.6 1.6 convert_element_type.21
  460.2 0.0 copy-done.3
  460.2 1.6 convert_element_type.24
  461.8 0.0 copy-done.2
  461.8 0.0 copy-start.1
  461.8 3.5 convert_element_type.25
  465.3 0.0 copy-done.1
  465.3 0.0 copy-start
  465.3 3.5 convert_element_type.26
  468.8 0.0 copy-done
  468.8 0.0 copy-start.6
  468.8 0.0 copy-start.5
  468.8 3.6 convert_element_type.27
  472.4 0.0 copy-done.6
  472.4 0.7 copy.30
  473.2 0.0 copy-done.5
  473.2 0.9 copy.31
  (1 shorter events, 0.0 us)
Async XLA Ops:
  451.6 7.1 %copy-start.4 = (bf16[512,1024]{1,0:T(8,128)(2,1)S(1)}, bf16[512,1024]{1,0:T(8,128)(2,1)}, u32[]{:S(2)}) copy-start(bf16[512,1024]{1,0:T(8,128)(2,1)} %get-tuple-element.50) | copy-start | bytes 3145732
  454.2 6.0 %copy-start.3 = (bf16[1024,512]{1,0:T(8,128)(2,1)S(1)}, bf16[1024,512]{1,0:T(8,128)(2,1)}, u32[]{:S(2)}) copy-start(bf16[1024,512]{1,0:T(8,128)(2,1)} %get-tuple-element.53) | copy-start | bytes 3145732
  458.6 3.2 copy-start.2
  461.8 3.5 copy-start.1
  465.3 3.5 copy-start
  468.8 3.6 copy-start.6
  468.8 4.4 copy-start.5

commit v4 on v3

--- a/solution.py
+++ b/solution.py
@@ -134,6 +134,7 @@
 def forward_kernel(
     rows_of,
     cols_of,
+    members,
     need,
     x,
     seg_row,
@@ -149,6 +150,7 @@
     gain2,
     wg,
     wu,
+    ct,
     n1,
     fs,
     raw,
@@ -161,6 +163,7 @@
     n2,
     hid,
     slope,
+    ct_all,
     unit,
     pq_own,
     pq_s,
@@ -179,6 +182,9 @@
     stat_recv,
     col_send,
     col_recv,
+    ct_send,
+    ct_recv,
+    ct_store,
 ):
     tokens, depth = x.shape
     width = depth * rows_of
@@ -188,7 +194,7 @@
     group = heads // key_heads
     scale = size ** (-0.5)
     me = lax.axis_index("row")
-    greet((("row", rows_of), ("col", cols_of)))
+    greet((("row", rows_of), ("col", cols_of), ("dp", members)))
 
     def row_exchange(kind, send, receive):
         return Exchange("row", rows_of, send, receive, row_send.at[kind], row_recv.at[kind])
@@ -236,6 +242,13 @@
         project(qkv.target(shift), pq_s, shift - 1)
         qkv.start(shift)
     project(me, pq_own, None)
+
+    need("ct")
+    spread = Ranked("dp", members, lambda shift: ct, ct_all, ct_send, ct_recv)
+    kept = pltpu.make_async_copy(ct, ct_all.at[spread.me], ct_store.at[0])
+    kept.start()
+    for shift in range(1, members):
+        spread.start(shift)
 
     def tables(rows, start, tile):
         key = lax.broadcasted_iota(jnp.int32, (tile, tokens), 1)
@@ -361,7 +374,10 @@
         slope[rows, fw:] = silu
 
     each_tile(tokens, activate)
-    for exchange in (stat1, qkv, gather, column, stat2, feed):
+    for shift in range(1, members):
+        spread.arrive(shift)
+    kept.wait()
+    for exchange in (stat1, qkv, gather, column, stat2, feed, spread):
         exchange.finish()
 
 
@@ -551,6 +567,96 @@
                 @pl.when(self.has_outer)
                 def _():
                     self.outward(index).wait_send()
+
+
+class Chain:
+    def __init__(self, members, own, blocks, send, receive, pass_send, pass_recv, row):
+        self.members, self.own, self.blocks, self.row = members, own, blocks, row
+        self.send, self.receive = send, receive
+        self.pass_send, self.pass_recv = pass_send, pass_recv
+        self.me = lax.axis_index("dp")
+
+    def valid(self, place):
+        return (place >= 0) & (place < self.members)
+
+    def step(self, side, hop):
+        way = 1 - 2 * side
+        origin = self.me - way * (hop - 1)
+        spot = self.blocks.at[origin, self.row.me]
+        return remote(
+            self.own if hop == 1 else spot,
+            spot,
+            self.send.at[side, hop - 1],
+            self.receive.at[side, hop - 1],
+            "dp",
+            self.me + way,
+        )
+
+    def incoming(self, side, hop):
+        origin = self.me - (1 - 2 * side) * hop
+        spot = self.blocks.at[origin, self.row.me]
+        return origin, remote(
+            spot,
+            spot,
+            self.send.at[side, hop - 1],
+            self.receive.at[side, hop - 1],
+            "dp",
+            self.me,
+        )
+
+    def sends(self, side, hop):
+        way = 1 - 2 * side
+        return self.valid(self.me - way * (hop - 1)) & self.valid(self.me + way)
+
+    def hop(self, hop):
+        for side in range(2):
+            if hop > 1:
+                self.await_block(side, hop - 1)
+
+            @pl.when(self.sends(side, hop))
+            def _(side=side):
+                self.step(side, hop).start()
+
+    def await_block(self, side, hop):
+        @pl.when(self.valid(self.me - (1 - 2 * side) * hop))
+        def _():
+            self.incoming(side, hop)[1].wait_recv()
+
+    def pass_on(self, side, hop, shift):
+        origin = self.me - (1 - 2 * side) * hop
+        spot = self.blocks.at[origin, self.row.me]
+        return remote(
+            spot,
+            spot,
+            self.pass_send.at[side, hop - 1, shift - 1],
+            self.pass_recv.at[side, hop - 1, shift - 1],
+            "row",
+            self.row.target(shift),
+        )
+
+    def spread(self, hop):
+        for side in range(2):
+            if hop == self.members - 1:
+                self.await_block(side, hop)
+
+            @pl.when(self.valid(self.me - (1 - 2 * side) * hop))
+            def _(side=side):
+                for shift in range(1, self.row.size):
+                    self.pass_on(side, hop, shift).start()
+
+    def finish(self):
+        for hop in range(1, self.members):
+            for side in range(2):
+
+                @pl.when(self.valid(self.me - (1 - 2 * side) * hop))
+                def _(side=side, hop=hop):
+                    for shift in range(1, self.row.size):
+                        self.pass_on(side, hop, shift).wait_recv()
+                        self.pass_on(side, hop, shift).wait_send()
+
+                @pl.when(self.sends(side, hop))
+                def _(side=side, hop=hop):
+                    self.step(side, hop).wait_send()
 
 
 def backward_kernel(
@@ -588,9 +694,10 @@
     small,
     *rest,
 ):
-    far, near, rest = rest[:7], rest[7:14], rest[14:]
-    grads, rest = rest[:7], rest[7:]
-    gq, gk, gv, go, gg, gu, gd = grads
+    hid_all, *rest = rest
+    far, near, rest = rest[:6], rest[6:12], rest[12:]
+    grads, rest = rest[:6], rest[6:]
+    gq, gk, gv, go, gg, gu = grads
     (
         gub,
         ph_s,
@@ -627,6 +734,11 @@
         out_send,
         store_sem,
         load_sem,
+        hop_send,
+        hop_recv,
+        pass_send,
+        pass_recv,
+        keep_sem,
         *spares,
     ) = rest
     tokens, depth = x.shape
@@ -678,35 +790,26 @@
 
     hide = row_exchange(0, lambda shift: hid, hid_r)
     gates = row_exchange(1, lambda shift: gub, gub_r)
-    for shift in range(1, rows_of):
-        hide.start(shift)
     body = pl.ds(0, tokens)
-    cut = ct[...]
+    chain = Chain(members, hid, hid_all, hop_send, hop_recv, pass_send, pass_recv, hide)
+    chain.hop(1)
     back = row_exchange(4, lambda shift: ph_s.at[shift - 1], ph_r)
-    for shift in range(rows_of):
-        if shift:
-            hide.arrive(shift)
-        piece = hid[...] if shift == 0 else hid_r[shift - 1]
-        index = window(hide.source(shift), fw)
-        part = dot(piece, wd[index, :])
-        if shift == 0:
-            ox_s[0, body, :] = part
-        else:
-            ox_s[0, body, :] += part
-        gd[index, :] = t_dot(piece, cut).astype(low)
-        line.release(6, hide.source(shift) * fw, fw, 0, depth)
-        if shift == 0:
-            for other in range(1, rows_of):
-                ph_s[other - 1] = dot_t(cut, wd[window(back.target(other), fw), :]).astype(low)
-                back.start(other)
-        else:
-            line.advance(1)
-    column0 = column_exchange(0)
-    for shift in range(1, cols_of):
-        column0.start(shift)
+    for shift in range(1, rows_of):
+        ph_s[shift - 1] = dot_t(ct[...], wd[window(back.target(shift), fw), :]).astype(low)
+        back.start(shift)
+    stage = lax.axis_index("dp")
+
+    def keep(shift):
+        piece = hid if shift == 0 else hid_r.at[shift - 1]
+        return pltpu.make_async_copy(
+            piece, hid_all.at[stage, hide.source(shift)], keep_sem.at[shift]
+        )
+
+    keep(0).start()
     n_t[...] = n2[...].T
     need("slope")
-    line.advance(2)
+    if members > 2:
+        chain.hop(2)
     for shift in range(1, rows_of):
         back.arrive(shift)
 
@@ -720,10 +823,12 @@
     each_tile(tokens, behind)
     for shift in range(1, rows_of):
         gates.start(shift)
+    for step in range(3, members):
+        chain.hop(step)
     need("wg", "wu")
     for shift in range(rows_of):
         if shift:
-            line.advance(2)
+            line.advance(1 if shift == 1 else 2)
             gates.arrive(shift)
         piece = gub if shift == 0 else gub_r.at[shift - 1]
         index = window(gates.source(shift), fw)
@@ -741,13 +846,6 @@
         column1.start(shift)
     line.advance(1)
     for shift in range(1, cols_of):
-        column0.arrive(shift)
-
-    def result(rows, start, tile):
-        bo[rows, :] = (mid[rows, :] + column_sum(0, rows)).astype(low)
-
-    each_tile(tokens, result)
-    for shift in range(1, cols_of):
         column1.arrive(shift)
 
     stat2 = stat_exchange(0)
@@ -846,6 +944,8 @@
     deliver = row_exchange(3, lambda shift: dqkv, dqkv_r)
     for shift in range(1, rows_of):
         deliver.start(shift)
+    for shift in range(1, rows_of):
+        hide.start(shift)
     need("wq", "wk", "wv")
     for shift in range(rows_of):
         if shift:
@@ -913,6 +1013,31 @@
         small_r[lax.axis_index("dp")] = small[...]
         for shift in range(1, members):
             ranked.start(shift)
+    line.advance(3)
+    for shift in range(rows_of):
+        if shift:
+            hide.arrive(shift)
+            keep(shift).start()
+        piece = hid[...] if shift == 0 else hid_r[shift - 1]
+        part = dot(piece, wd[window(hide.source(shift), fw), :])
+        if shift == 0:
+            ox_s[0, body, :] = part
+        else:
+            ox_s[0, body, :] += part
+    column0 = column_exchange(0)
+    for shift in range(1, cols_of):
+        column0.start(shift)
+    for step in range(1, members):
+        chain.spread(step)
+    line.advance(1)
+    for shift in range(1, cols_of):
+        column0.arrive(shift)
+
+    def result(rows, start, tile):
+        bo[rows, :] = (mid[rows, :] + column_sum(0, rows)).astype(low)
+
+    each_tile(tokens, result)
+    if members > 1:
         line.settle()
         for shift in range(1, members):
             ranked.arrive(shift)
@@ -921,8 +1046,51 @@
         for member in range(1, members):
             summed = summed + small_r[member]
         small[...] = summed
+    chain.finish()
+    for shift in range(rows_of):
+        keep(shift).wait()
     for exchange in (hide, back, gates, column0, column1, stat2, deliver, column2, stat1):
         exchange.finish()
+
+
+def widen_kernel(*refs):
+    count = (len(refs) - 3) // 2
+    hid_all, ct_all = refs[count : count + 2]
+    *out, gd = refs[count + 2 :]
+    for source, target in zip(refs[:count], out):
+        target[...] = source[...].astype(wide)
+    total = t_dot(hid_all[0, 0], ct_all[0])
+    for member in range(1, ct_all.shape[0]):
+        total = total + t_dot(hid_all[member, 0], ct_all[member])
+    gd[...] = total
+
+
+def widen(partials, hid_all, ct_all, shape):
+    members, rows_of, tokens, fw = hid_all.shape
+    parts = 2 if fw % (2 * lanes) == 0 else 1
+    steps = rows_of * parts
+
+    def rows(array_shape):
+        return pl.BlockSpec((array_shape[0] // steps, array_shape[1]), lambda i: (i, 0))
+
+    specs = [rows(partial_sum.shape) for partial_sum in partials]
+    return pl.pallas_call(
+        widen_kernel,
+        grid=(steps,),
+        out_shape=tuple(
+            jax.ShapeDtypeStruct(array_shape, wide)
+            for array_shape in [*(partial_sum.shape for partial_sum in partials), shape]
+        ),
+        in_specs=specs
+        + [
+            pl.BlockSpec(
+                (members, 1, tokens, fw // parts), lambda i: (0, i // parts, 0, i % parts)
+            ),
+            pl.BlockSpec(ct_all.shape, lambda i: (0, 0, 0)),
+        ],
+        out_specs=tuple(specs + [rows(shape)]),
+        compiler_params=pltpu.CompilerParams(vmem_limit_bytes=full_vmem),
+    )(*partials, hid_all, ct_all)
 
 
 def vmem(shape, kind):
@@ -1003,6 +1171,7 @@
     gain1, gain2 = attention_norm[None, :], feedforward_norm[None, :]
     qn, kn = query_norm[None, :], key_norm[None, :]
     total = qw + 2 * kw
+    peers = max(members - 1, 1)
     dma = pltpu.SemaphoreType.DMA
 
     def sems(kinds):
@@ -1016,7 +1185,7 @@
         ]
 
     saved = call(
-        partial(forward_kernel, rows_of, cols_of),
+        partial(forward_kernel, rows_of, cols_of, members),
         (
             ((tokens, depth), low),
             ((tokens, lanes), wide),
@@ -1030,6 +1199,7 @@
             ((tokens, depth), low),
             ((tokens, fw), low),
             ((tokens, 2 * fw), wide),
+            ((members, tokens, depth), low),
         ),
         [
             vmem((tokens, depth), low),
@@ -1045,7 +1215,8 @@
             vmem((tokens, depth), wide),
             vmem((beside, tokens, depth), wide),
         ]
-        + sems(1),
+        + sems(1)
+        + [dma((peers,)), dma((peers,)), dma((1,))],
         0,
         dict(
             x=block_input,
@@ -1062,16 +1233,18 @@
             gain2=gain2,
             wg=gate_weight,
             wu=up_weight,
+            ct=cotangent,
         ),
-        late=("wo", "wg", "wu"),
+        late=("wo", "wg", "wu", "ct"),
+        outside=(12,),
     )
+    *saved, ct_all = saved
     saved = dict(
         zip(("n1", "fs", "raw", "lows", "shares", "trig", "mixed", "mid", "ss", "n2", "hid", "slope"), saved)
     )
     weights = (query_weight, key_weight, value_weight, output_weight, gate_weight, up_weight)
-    shapes = [weight.shape for weight in weights] + [down_weight.shape]
+    shapes = [weight.shape for weight in weights]
     pieces = {
-        (fw, depth): rows_of,
         (depth, fw): 2 * rows_of,
         (qw, depth): rows_of,
         (depth, qw * rows_of): 1,
@@ -1079,13 +1252,13 @@
     }
     slots = sum(split(*shape) * times for shape, times in pieces.items())
     spares = {(shape[0] // split(*shape), shape[1]) for shape in pieces}
-    peers = max(members - 1, 1)
     done = call(
         partial(backward_kernel, rows_of, cols_of, members),
         (
             ((tokens, depth), low),
             ((tokens, depth), wide),
             ((16, depth), wide),
+            ((members, rows_of, tokens, fw), low),
             *((shape, low) for shape in shapes * 2),
         ),
         [vmem(shape, low) for shape in shapes]
@@ -1115,6 +1288,9 @@
         + [vmem((members, 16, depth), wide), dma((peers,)), dma((peers,))]
         + [dma((slots,))] * 5
         + [dma((2,))]
+        + [dma((2, peers))] * 2
+        + [dma((2, peers, others))] * 2
+        + [dma((rows_of,))]
         + [vmem((2, *shape), low) for shape in sorted(spares)],
         1,
         dict(
@@ -1134,10 +1310,10 @@
             wd=down_weight,
         ),
         late=("x", "n1", "fs", "raw", "lows", "shares", "trig", "mixed", "slope", "wq", "wk", "wv", "wo", "wg", "wu"),
-        outside=range(3, 17),
+        outside=range(3, 16),
     )
-    block_output, input_gradient, small, *partials = done[:10]
-    gq, gk, gv, go, gg, gu, gd = (partial_sum.astype(wide) for partial_sum in partials)
+    block_output, input_gradient, small, hid_all, *partials = done[:10]
+    gq, gk, gv, go, gg, gu, gd = widen(partials, hid_all, ct_all, down_weight.shape)
     return (
         block_output,
         input_gradient,

time: 476 us -> 439 us (0.922)
  Pallas kernels: 449 us -> 428 us
  other arithmetic: 18.8 us -> 0.6 us
    pallas_call x2, Pallas kernels: 449 us -> 408 us  [call(): pl.pallas_call(body, out_shape=tuple((jax.ShapeDtypeStruct(shape, kind) f...]
    pallas_call x0 -> x1, Pallas kernels: none -> 20.4 us  [widen(): pl.pallas_call(widen_kernel, grid=(steps,), out_shape=tuple((jax.ShapeDty...]
    convert_element_type x7 -> x0, other arithmetic: 18.2 us -> none  [per_device(): partial_sum.astype(wide)]
where the time goes in v4:
time: 439 us; the launch traced here: 437 us
  Pallas kernels  428 us (97%)
  local copies, waits for them, and re-layouts  7.97 us (2%)
    pallas_call x2, Pallas kernels, call(): pl.pallas_call(body, out_shape=tuple((jax.ShapeDtypeStruct(shape, kind) f...  408 us
    pallas_call x1, Pallas kernels, widen(): pl.pallas_call(widen_kernel, grid=(steps,), out_shape=tuple((jax.ShapeDty...  20.4 us

profile of v4, /device:TPU:0, one launch (start us, length us, event | category | flops | bytes accessed | tf_op | source)
XLA Modules:
  0.0 437.2 jit_solution(789390505530915005)
XLA Ops:
  0.7 0.6 maximum_bitcast_fusion.refs_3_
  1.2 1.5 copy.27.refs_2_
  2.7 115.6 %shard_map.237 = (bf16[384,512]{1,0:T(8,128)(2,1)}, f32[384,128]{1,0:T(8,128)}, f32[384,384]{1,0:T(8,128)}, bf16[384,512]{1,0:T(8,128)(2,1)}, f32[2,384,384]{2,1...) custom-call(bf16[384,512]{1,0:T(8,128)(2,1)} %refs_0_.3, ...), custom_call_target="tpu_custom_call" | custom-call | tf_op jit(solution)/shard_map/pallas_call | solution.py:1130
  118.3 292.0 %shard_map.238 = (bf16[384,512]{1,0:T(8,128)(2,1)}, f32[384,512]{1,0:T(8,128)}, f32[16,512]{1,0:T(8,128)}, bf16[4,4,384,768]{3,2,1,0:T(8,128)(2,1)}, bf16[512,10...) custom-call(bf16[384,512]{1,0:T(8,128)(2,1)} %refs_0_.3, ...), custom_call_target="tpu_custom_call" | custom-call | tf_op jit(solution)/shard_map/pallas_call | solution.py:1130
  410.3 1.3 slice_bitcast_fusion
  411.6 1.4 fusion
  413.0 20.4 %shard_map.239 = (f32[512,1024]{1,0:T(8,128)}, f32[512,512]{1,0:T(8,128)}, f32[512,512]{1,0:T(8,128)}, f32[1024,512]{1,0:T(8,128)}, f32[512,3072]{1,0:T(8,128)},...) custom-call(bf16[512,1024]{1,0:T(8,128)(2,1)} %get-tuple-element.58.refs_0_, bf16[512,512]{1,0:T(8,128)(2,1)} %get-tuple-element.59.refs_1_, ...), custom_call_target="tpu_custom_call" | custom-call | tf_op jit(solution)/shard_map/pallas_call | solution.py:1077
  433.4 1.8 copy.30
  435.2 2.1 copy.31
  (1 shorter events, 0.0 us)

commit v5 on v4

--- a/solution.py
+++ b/solution.py
@@ -11,8 +11,11 @@
 rope_base = 1000000.0
 lanes = 128
 full_vmem = 67043328
-chunk_limit = 262144
-lag = 2
+chunk_limit = 131072
+lag = 3
+pace = 2
+bulk = 6
+slots_left = 1000
 low = jnp.bfloat16
 wide = jnp.float32
 
@@ -119,6 +122,89 @@
         for member in range(1, self.size):
             result = result + self.receive[member, rows]
         return result
+
+
+class Reduce:
+    def __init__(self, size, produce, send, receive, extra, send_sem, receive_sem):
+        self.size, self.produce = size, produce
+        self.send, self.receive, self.extra = send, receive, extra
+        self.send_sem, self.receive_sem = send_sem, receive_sem
+        self.halved = size == 4
+        self.count = 2 if self.halved else size - 1
+        me = lax.axis_index("row")
+        if self.halved:
+            self.half = send.shape[1] // 2
+            beside = me + 1 - 2 * lax.rem(me, 2)
+            across = lax.rem(me + 2, 4)
+            self.members = (beside, across, lax.rem(beside + 2, 4))
+        else:
+            self.direct = Exchange(
+                "row", size, lambda shift: send.at[shift - 1], receive, send_sem, receive_sem
+            )
+
+    def rows(self, part):
+        return pl.ds(part * self.half, self.half)
+
+    def copy(self, kind):
+        slot, part, to = ((2, 0, 0), (2, 1, 1), (0, 0, 0), (1, 1, 1), (0, 1, 0), (1, 0, 1))[kind]
+        source = self.send.at[slot, self.rows(part)]
+        target = self.extra.at[to] if slot == 2 else self.receive.at[slot, self.rows(part)]
+        return remote(
+            source,
+            target,
+            self.send_sem.at[kind],
+            self.receive_sem.at[kind],
+            "row",
+            self.members[to],
+        )
+
+    def start(self):
+        if not self.halved:
+            for shift in range(1, self.size):
+                self.produce(self.direct.target(shift), shift - 1)
+                self.direct.start(shift)
+            return
+        self.produce(self.members[2], 2)
+        self.copy(0).start()
+        self.copy(1).start()
+        self.produce(self.members[0], 0)
+        self.copy(2).start()
+        self.produce(self.members[1], 1)
+        self.copy(3).start()
+
+    def relay(self):
+        if not self.halved:
+            return
+        for kind, slot in ((0, 1), (1, 0)):
+            self.copy(kind).wait_recv()
+            tile = 32 if self.half % 32 == 0 else self.half
+
+            def step(index, carry, kind=kind, slot=slot, tile=tile):
+                spot = pl.ds(pl.multiple_of(index * tile, 16), tile)
+                rows = pl.ds(pl.multiple_of(kind * self.half + index * tile, 16), tile)
+                total = self.send[slot, rows, :].astype(wide) + self.extra[kind, spot, :].astype(
+                    wide
+                )
+                self.send[slot, rows, :] = total.astype(low)
+                return carry
+
+            lax.fori_loop(0, self.half // tile, step, 0)
+            self.copy(5 - kind).start()
+
+    def arrive(self):
+        if not self.halved:
+            for shift in range(1, self.size):
+                self.direct.arrive(shift)
+            return
+        for kind in range(2, 6):
+            self.copy(kind).wait_recv()
+
+    def finish(self):
+        if not self.halved:
+            self.direct.finish()
+            return
+        for kind in range(6):
+            self.copy(kind).wait_send()
 
 
 def each_tile(rows, body):
@@ -168,9 +254,11 @@
     pq_own,
     pq_s,
     pq_r,
+    pq_x,
     pg_own,
     pg_s,
     pg_r,
+    pg_x,
     mixed_r,
     stat_s,
     stat_r,
@@ -185,6 +273,8 @@
     ct_send,
     ct_recv,
     ct_store,
+    sum_send,
+    sum_recv,
 ):
     tokens, depth = x.shape
     width = depth * rows_of
@@ -237,11 +327,18 @@
             target[slot, :, qw : qw + kw] = k.astype(kind)
             target[slot, :, qw + kw :] = v.astype(kind)
 
-    qkv = row_exchange(0, lambda shift: pq_s.at[shift - 1], pq_r)
-    for shift in range(1, rows_of):
-        project(qkv.target(shift), pq_s, shift - 1)
-        qkv.start(shift)
+    qkv = Reduce(
+        rows_of,
+        lambda index, slot: project(index, pq_s, slot),
+        pq_s,
+        pq_r,
+        pq_x,
+        sum_send.at[0],
+        sum_recv.at[0],
+    )
+    qkv.start()
     project(me, pq_own, None)
+    qkv.relay()
 
     need("ct")
     spread = Ranked("dp", members, lambda shift: ct, ct_all, ct_send, ct_recv)
@@ -263,7 +360,7 @@
 
     for shift in range(1, rows_of):
         stat1.arrive(shift)
-        qkv.arrive(shift)
+    qkv.arrive()
 
     def heads_in(rows, start, tile):
         first = lax.rsqrt(stat1.total(rows) / width + epsilon)
@@ -271,8 +368,8 @@
         first = first[:, :1]
         n1[rows, :] = (x[rows, :].astype(wide) * first * gain1[...]).astype(low)
         value = pq_own[rows, :]
-        for shift in range(1, rows_of):
-            value = value + pq_r[shift - 1, rows, :].astype(wide)
+        for slot in range(qkv.count):
+            value = value + pq_r[slot, rows, :].astype(wide)
         value = value * first
         raw[rows, :] = value[:, : qw + kw]
         cosine, sine = trig[0, rows, :], trig[1, rows, :]
@@ -338,12 +435,13 @@
         stat2.start(shift)
 
     need("wg", "wu")
-    feed = row_exchange(3, lambda shift: pg_s.at[shift - 1], pg_r)
-    for shift in range(1, rows_of):
-        columns = window(feed.target(shift), fw)
-        pg_s[shift - 1, :, :fw] = dot(unit[...], wg[:, columns]).astype(low)
-        pg_s[shift - 1, :, fw:] = dot(unit[...], wu[:, columns]).astype(low)
-        feed.start(shift)
+    def widen_out(index, slot):
+        columns = window(index, fw)
+        pg_s[slot, :, :fw] = dot(unit[...], wg[:, columns]).astype(low)
+        pg_s[slot, :, fw:] = dot(unit[...], wu[:, columns]).astype(low)
+
+    feed = Reduce(rows_of, widen_out, pg_s, pg_r, pg_x, sum_send.at[1], sum_recv.at[1])
+    feed.start()
     pg_own[:, :fw] = dot(unit[...], wg[:, window(me, fw)])
     pg_own[:, fw:] = dot(unit[...], wu[:, window(me, fw)])
     for shift in range(1, rows_of):
@@ -355,16 +453,16 @@
         n2[rows, :] = (mid[rows, :] * second[:, :1] * gain2[...]).astype(low)
 
     each_tile(tokens, scale_rows)
-    for shift in range(1, rows_of):
-        feed.arrive(shift)
+    feed.relay()
+    feed.arrive()
 
     def activate(rows, start, tile):
         second = ss[rows, :1]
         gate = pg_own[rows, :fw]
         upward = pg_own[rows, fw:]
-        for shift in range(1, rows_of):
-            gate = gate + pg_r[shift - 1, rows, :fw].astype(wide)
-            upward = upward + pg_r[shift - 1, rows, fw:].astype(wide)
+        for slot in range(feed.count):
+            gate = gate + pg_r[slot, rows, :fw].astype(wide)
+            upward = upward + pg_r[slot, rows, fw:].astype(wide)
         gate = gate * second
         upward = upward * second
         sigmoid = jax.nn.sigmoid(gate)
@@ -516,6 +614,8 @@
         if self.members == 1:
             return
         for _ in range(count):
+            if self.done == len(self.chunks):
+                return
             index = self.done
             self.done += 1
 
@@ -828,7 +928,7 @@
     need("wg", "wu")
     for shift in range(rows_of):
         if shift:
-            line.advance(1 if shift == 1 else 2)
+            line.advance(pace * (1 if shift == 1 else 2))
             gates.arrive(shift)
         piece = gub if shift == 0 else gub_r.at[shift - 1]
         index = window(gates.source(shift), fw)
@@ -844,7 +944,7 @@
     column1 = column_exchange(1)
     for shift in range(1, cols_of):
         column1.start(shift)
-    line.advance(1)
+    line.advance(1 * pace)
     for shift in range(1, cols_of):
         column1.arrive(shift)
 
@@ -867,7 +967,7 @@
     for shift in range(1, rows_of):
         stat2.start(shift)
     need("wo", "mixed", "lows", "shares")
-    line.advance(1)
+    line.advance(1 * pace)
     for shift in range(1, rows_of):
         stat2.arrive(shift)
 
@@ -891,7 +991,7 @@
         index = window(blend.source(shift), qw)
         go[index, :] = t_dot(mixed[shift], ml[...]).astype(low)
         line.release(3, blend.source(shift) * qw, qw, 0, depth)
-    line.advance(2)
+    line.advance(2 * pace)
     for shift in range(1, rows_of):
         blend.arrive(shift)
 
@@ -915,7 +1015,7 @@
     each_tile(tokens, share_back)
     need("n1", "raw", "trig")
     n_t[...] = n1[...].T
-    line.advance(1)
+    line.advance(1 * pace)
 
     def pull(head, back, gain, row):
         raw_piece = raw[:, head * size : (head + 1) * size]
@@ -946,10 +1046,12 @@
         deliver.start(shift)
     for shift in range(1, rows_of):
         hide.start(shift)
+    if members > 1:
+        chain.spread(1)
     need("wq", "wk", "wv")
     for shift in range(rows_of):
         if shift:
-            line.advance(1)
+            line.advance(1 * pace)
             deliver.arrive(shift)
         piece = dqkv if shift == 0 else dqkv_r.at[shift - 1]
         source = deliver.source(shift)
@@ -974,7 +1076,7 @@
     line.release(0, 0, depth, 0, qw * rows_of)
     line.release(1, 0, depth, 0, kw * rows_of)
     line.release(2, 0, depth, 0, kw * rows_of)
-    line.advance(1)
+    line.advance(1 * pace)
     for shift in range(1, cols_of):
         column2.arrive(shift)
     need("x", "fs")
@@ -996,24 +1098,9 @@
     stat_r[1, me, pad] = summed
     for shift in range(1, rows_of):
         stat1.start(shift)
-    line.advance(1)
-    for shift in range(1, rows_of):
-        stat1.arrive(shift)
-
-    def finish(rows, start, tile):
-        first = fs[rows, :1]
-        unit = x[rows, :].astype(wide) * first
-        inner = stat1.total(rows)[:, :1] / width
-        ig[rows, :] = mb[rows, :] + first * (column_sum(2, rows) * gain1[...] - unit * inner)
-
-    each_tile(tokens, finish)
-    small[8:16, :lanes] = stat1.total(pad)
-    ranked = Ranked("dp", members, lambda shift: small, small_r, small_send, small_recv)
-    if members > 1:
-        small_r[lax.axis_index("dp")] = small[...]
-        for shift in range(1, members):
-            ranked.start(shift)
-    line.advance(3)
+    for step in range(2, members):
+        chain.spread(step)
+    line.advance(bulk * pace)
     for shift in range(rows_of):
         if shift:
             hide.arrive(shift)
@@ -1027,9 +1114,6 @@
     column0 = column_exchange(0)
     for shift in range(1, cols_of):
         column0.start(shift)
-    for step in range(1, members):
-        chain.spread(step)
-    line.advance(1)
     for shift in range(1, cols_of):
         column0.arrive(shift)
 
@@ -1037,6 +1121,23 @@
         bo[rows, :] = (mid[rows, :] + column_sum(0, rows)).astype(low)
 
     each_tile(tokens, result)
+    line.advance(slots_left)
+    for shift in range(1, rows_of):
+        stat1.arrive(shift)
+
+    def finish(rows, start, tile):
+        first = fs[rows, :1]
+        unit = x[rows, :].astype(wide) * first
+        inner = stat1.total(rows)[:, :1] / width
+        ig[rows, :] = mb[rows, :] + first * (column_sum(2, rows) * gain1[...] - unit * inner)
+
+    each_tile(tokens, finish)
+    small[8:16, :lanes] = stat1.total(pad)
+    ranked = Ranked("dp", members, lambda shift: small, small_r, small_send, small_recv)
+    if members > 1:
+        small_r[lax.axis_index("dp")] = small[...]
+        for shift in range(1, members):
+            ranked.start(shift)
     if members > 1:
         line.settle()
         for shift in range(1, members):
@@ -1058,14 +1159,14 @@
     hid_all, ct_all = refs[count : count + 2]
     *out, gd = refs[count + 2 :]
     for source, target in zip(refs[:count], out):
-        target[...] = source[...].astype(wide)
+        target[...] = source[...].astype(target.dtype)
     total = t_dot(hid_all[0, 0], ct_all[0])
     for member in range(1, ct_all.shape[0]):
         total = total + t_dot(hid_all[member, 0], ct_all[member])
     gd[...] = total
 
 
-def widen(partials, hid_all, ct_all, shape):
+def widen(arrays, kinds, hid_all, ct_all, shape):
     members, rows_of, tokens, fw = hid_all.shape
     parts = 2 if fw % (2 * lanes) == 0 else 1
     steps = rows_of * parts
@@ -1073,14 +1174,12 @@
     def rows(array_shape):
         return pl.BlockSpec((array_shape[0] // steps, array_shape[1]), lambda i: (i, 0))
 
-    specs = [rows(partial_sum.shape) for partial_sum in partials]
+    specs = [rows(array.shape) for array in arrays]
+    shapes = [array.shape for array in arrays] + [shape]
     return pl.pallas_call(
         widen_kernel,
         grid=(steps,),
-        out_shape=tuple(
-            jax.ShapeDtypeStruct(array_shape, wide)
-            for array_shape in [*(partial_sum.shape for partial_sum in partials), shape]
-        ),
+        out_shape=tuple(map(jax.ShapeDtypeStruct, shapes, kinds)),
         in_specs=specs
         + [
             pl.BlockSpec(
@@ -1090,7 +1189,7 @@
         ],
         out_specs=tuple(specs + [rows(shape)]),
         compiler_params=pltpu.CompilerParams(vmem_limit_bytes=full_vmem),
-    )(*partials, hid_all, ct_all)
+    )(*arrays, hid_all, ct_all)
 
 
 def vmem(shape, kind):
@@ -1206,9 +1305,11 @@
             vmem((tokens, total), wide),
             vmem((others, tokens, total), low),
             vmem((others, tokens, total), low),
+            vmem((2, tokens // 2, total), low),
             vmem((tokens, 2 * fw), wide),
             vmem((others, tokens, 2 * fw), low),
             vmem((others, tokens, 2 * fw), low),
+            vmem((2, tokens // 2, 2 * fw), low),
             vmem((others, tokens, qw), low),
             vmem((2, tokens, lanes), wide),
             vmem((2, rows_of, tokens, lanes), wide),
@@ -1216,7 +1317,8 @@
             vmem((beside, tokens, depth), wide),
         ]
         + sems(1)
-        + [dma((peers,)), dma((peers,)), dma((1,))],
+        + [dma((peers,)), dma((peers,)), dma((1,))]
+        + [dma((2, max(6, others)))] * 2,
         0,
         dict(
             x=block_input,
@@ -1313,7 +1415,13 @@
         outside=range(3, 16),
     )
     block_output, input_gradient, small, hid_all, *partials = done[:10]
-    gq, gk, gv, go, gg, gu, gd = widen(partials, hid_all, ct_all, down_weight.shape)
+    block_output, input_gradient, gq, gk, gv, go, gg, gu, gd = widen(
+        (block_output, input_gradient, *partials),
+        [low] + [wide] * 8,
+        hid_all,
+        ct_all,
+        down_weight.shape,
+    )
     return (
         block_output,
         input_gradient,

time: 439 us -> 415 us (0.945)
  Pallas kernels: 428 us -> 407 us
    pallas_call x2, Pallas kernels: 408 us -> 386 us  [call(): pl.pallas_call(body, out_shape=tuple((jax.ShapeDtypeStruct(shape, kind) f...]
where the time goes in v5:
time: 415 us; the launch traced here: 413 us
  Pallas kernels  407 us (98%)
    pallas_call x2, Pallas kernels, call(): pl.pallas_call(body, out_shape=tuple((jax.ShapeDtypeStruct(shape, kind) f...  386 us
    pallas_call x1, Pallas kernels, widen(): pl.pallas_call(widen_kernel, grid=(steps,), out_shape=tuple(map(jax.Shape...  21.2 us

profile of v5, /device:TPU:0, one launch (start us, length us, event | category | flops | bytes accessed | tf_op | source)
XLA Modules:
  0.0 412.9 jit_solution(570608816438648442)
XLA Ops:
  0.7 0.6 maximum_bitcast_fusion.refs_3_
  1.2 1.5 copy.27.refs_2_
  2.7 98.7 %shard_map.237 = (bf16[384,512]{1,0:T(8,128)(2,1)}, f32[384,128]{1,0:T(8,128)}, f32[384,384]{1,0:T(8,128)}, bf16[384,512]{1,0:T(8,128)(2,1)}, f32[2,384,384]{2,1...) custom-call(bf16[384,512]{1,0:T(8,128)(2,1)} %refs_0_.3, ...), custom_call_target="tpu_custom_call" | custom-call | tf_op jit(solution)/shard_map/pallas_call | solution.py:1229
  101.5 287.4 %shard_map.238 = (bf16[384,512]{1,0:T(8,128)(2,1)}, f32[384,512]{1,0:T(8,128)}, f32[16,512]{1,0:T(8,128)}, bf16[4,4,384,768]{3,2,1,0:T(8,128)(2,1)}, bf16[512,10...) custom-call(bf16[384,512]{1,0:T(8,128)(2,1)} %refs_0_.3, ...), custom_call_target="tpu_custom_call" | custom-call | tf_op jit(solution)/shard_map/pallas_call | solution.py:1229
  388.9 1.3 slice_bitcast_fusion
  390.2 1.4 fusion
  391.5 21.2 %shard_map.239 = (bf16[384,512]{1,0:T(8,128)(2,1)}, f32[384,512]{1,0:T(8,128)}, f32[512,1024]{1,0:T(8,128)}, f32[512,512]{1,0:T(8,128)}, f32[512,512]{1,0:T(8,12...) custom-call(bf16[384,512]{1,0:T(8,128)(2,1)} %get-tuple-element.57.refs_0_, ...), custom_call_target="tpu_custom_call" | custom-call | tf_op jit(solution)/shard_map/pallas_call | solution.py:1179
  (1 shorter events, 0.0 us)

commit v6 on v5

--- a/solution.py
+++ b/solution.py
@@ -2,6 +2,7 @@
 
 import jax
 import jax.numpy as jnp
+import numpy as np
 from jax import lax
 from jax.experimental import pallas as pl
 from jax.experimental.pallas import tpu as pltpu
@@ -224,7 +225,6 @@
     need,
     x,
     seg_row,
-    seg_col,
     inverse,
     gain1,
     wq,
@@ -237,6 +237,7 @@
     wg,
     wu,
     ct,
+    wd,
     n1,
     fs,
     raw,
@@ -248,13 +249,18 @@
     ss,
     n2,
     hid,
-    slope,
+    gub,
     ct_all,
+    seg_col,
     unit,
     pq_own,
     pq_s,
     pq_r,
     pq_x,
+    ph_own,
+    ph_s,
+    ph_r,
+    ph_x,
     pg_own,
     pg_s,
     pg_r,
@@ -339,18 +345,27 @@
     qkv.start()
     project(me, pq_own, None)
     qkv.relay()
-
-    need("ct")
+    need("ct", "wd")
+
+    def behind_out(index, slot):
+        ph_s[slot] = dot_t(ct[...], wd[window(index, fw), :]).astype(low)
+
+    back = Reduce(rows_of, behind_out, ph_s, ph_r, ph_x, sum_send.at[2], sum_recv.at[2])
+    back.start()
+    ph_own[...] = dot_t(ct[...], wd[window(me, fw), :])
     spread = Ranked("dp", members, lambda shift: ct, ct_all, ct_send, ct_recv)
     kept = pltpu.make_async_copy(ct, ct_all.at[spread.me], ct_store.at[0])
     kept.start()
     for shift in range(1, members):
         spread.start(shift)
 
+    line = seg_row[...].astype(wide)
+    seg_col[...] = jnp.broadcast_to(line, (lanes, tokens)).T
+
     def tables(rows, start, tile):
         key = lax.broadcasted_iota(jnp.int32, (tile, tokens), 1)
         query = lax.broadcasted_iota(jnp.int32, (tile, tokens), 0) + start
-        allowed = (seg_col[rows, :] == seg_row[...]) & (key <= query)
+        allowed = (seg_col[rows, :1] == seg_row[...].astype(wide)) & (key <= query)
         count = jnp.sum(jnp.where(allowed, 1.0, 0.0), axis=1, keepdims=True) - 1.0
         angle = count * inverse[...]
         trig[0, rows, :] = jnp.cos(angle)
@@ -387,7 +402,7 @@
     def attend(rows, start, tile):
         key = lax.broadcasted_iota(jnp.int32, (tile, tokens), 1)
         query = lax.broadcasted_iota(jnp.int32, (tile, tokens), 0) + start
-        allowed = (seg_col[rows, :] == seg_row[...]) & (key <= query)
+        allowed = (seg_col[rows, :1] == seg_row[...].astype(wide)) & (key <= query)
         for head in range(heads):
             pair = head // group
             keys = lows[:, qw + pair * size : qw + (pair + 1) * size]
@@ -407,6 +422,7 @@
         gather.start(shift)
     need("wo")
     ox_s[...] = dot(mixed[0], wo[window(me, qw), :])
+    back.relay()
     for shift in range(1, rows_of):
         gather.arrive(shift)
         mixed[shift] = mixed_r[shift - 1]
@@ -455,6 +471,7 @@
     each_tile(tokens, scale_rows)
     feed.relay()
     feed.arrive()
+    back.arrive()
 
     def activate(rows, start, tile):
         second = ss[rows, :1]
@@ -468,14 +485,17 @@
         sigmoid = jax.nn.sigmoid(gate)
         silu = gate * sigmoid
         hid[rows, :] = (silu * upward).astype(low)
-        slope[rows, :fw] = upward * sigmoid * (1.0 + gate * (1.0 - sigmoid))
-        slope[rows, fw:] = silu
+        behind = ph_own[rows, :]
+        for slot in range(back.count):
+            behind = behind + ph_r[slot, rows, :].astype(wide)
+        gub[rows, :fw] = (behind * upward * sigmoid * (1.0 + gate * (1.0 - sigmoid))).astype(low)
+        gub[rows, fw:] = (behind * silu).astype(low)
 
     each_tile(tokens, activate)
     for shift in range(1, members):
         spread.arrive(shift)
     kept.wait()
-    for exchange in (stat1, qkv, gather, column, stat2, feed, spread):
+    for exchange in (stat1, qkv, back, gather, column, stat2, feed, spread):
         exchange.finish()
 
 
@@ -777,7 +797,7 @@
     ss,
     n2,
     hid,
-    slope,
+    gub,
     gain1,
     gain2,
     qn,
@@ -799,9 +819,6 @@
     grads, rest = rest[:6], rest[6:]
     gq, gk, gv, go, gg, gu = grads
     (
-        gub,
-        ph_s,
-        ph_r,
         hid_r,
     gub_r,
     n_t,
@@ -893,10 +910,8 @@
     body = pl.ds(0, tokens)
     chain = Chain(members, hid, hid_all, hop_send, hop_recv, pass_send, pass_recv, hide)
     chain.hop(1)
-    back = row_exchange(4, lambda shift: ph_s.at[shift - 1], ph_r)
     for shift in range(1, rows_of):
-        ph_s[shift - 1] = dot_t(ct[...], wd[window(back.target(shift), fw), :]).astype(low)
-        back.start(shift)
+        gates.start(shift)
     stage = lax.axis_index("dp")
 
     def keep(shift):
@@ -907,28 +922,12 @@
 
     keep(0).start()
     n_t[...] = n2[...].T
-    need("slope")
-    if members > 2:
-        chain.hop(2)
-    for shift in range(1, rows_of):
-        back.arrive(shift)
-
-    def behind(rows, start, tile):
-        value = dot_t(ct[rows, :], wd[window(me, fw), :])
-        for shift in range(1, rows_of):
-            value = value + ph_r[shift - 1, rows, :].astype(wide)
-        gub[rows, :fw] = (value * slope[rows, :fw]).astype(low)
-        gub[rows, fw:] = (value * slope[rows, fw:]).astype(low)
-
-    each_tile(tokens, behind)
-    for shift in range(1, rows_of):
-        gates.start(shift)
-    for step in range(3, members):
-        chain.hop(step)
     need("wg", "wu")
     for shift in range(rows_of):
         if shift:
             line.advance(pace * (1 if shift == 1 else 2))
+            if shift + 1 < members:
+                chain.hop(shift + 1)
             gates.arrive(shift)
         piece = gub if shift == 0 else gub_r.at[shift - 1]
         index = window(gates.source(shift), fw)
@@ -941,6 +940,9 @@
         line.release(4, 0, depth, gates.source(shift) * fw, fw)
         gu[:, index] = dot(n_t[...], piece[:, fw:]).astype(low)
         line.release(5, 0, depth, gates.source(shift) * fw, fw)
+    for step in range(rows_of + 1, members):
+        chain.hop(step)
+    need("mid", "ss")
     column1 = column_exchange(1)
     for shift in range(1, cols_of):
         column1.start(shift)
@@ -966,7 +968,7 @@
     stat_s[0, pad] = jnp.zeros((8, lanes), wide)
     for shift in range(1, rows_of):
         stat2.start(shift)
-    need("wo", "mixed", "lows", "shares")
+    need("wo", "mixed", "lows", "shares", "ct")
     line.advance(1 * pace)
     for shift in range(1, rows_of):
         stat2.arrive(shift)
@@ -1101,6 +1103,7 @@
     for step in range(2, members):
         chain.spread(step)
     line.advance(bulk * pace)
+    need("wd")
     for shift in range(rows_of):
         if shift:
             hide.arrive(shift)
@@ -1150,14 +1153,18 @@
     chain.finish()
     for shift in range(rows_of):
         keep(shift).wait()
-    for exchange in (hide, back, gates, column0, column1, stat2, deliver, column2, stat1):
+    for exchange in (hide, gates, column0, column1, stat2, deliver, column2, stat1):
         exchange.finish()
 
 
 def widen_kernel(*refs):
-    count = (len(refs) - 3) // 2
-    hid_all, ct_all = refs[count : count + 2]
-    *out, gd = refs[count + 2 :]
+    count = (len(refs) - 8) // 2
+    hid_all, ct_all, small = refs[count : count + 3]
+    *out, gd, gain1, gain2, gain_q, gain_k = refs[count + 3 :]
+    gain1[...] = small[0:1, :]
+    gain2[...] = small[1:2, :]
+    gain_q[...] = small[8:9, : gain_q.shape[1]]
+    gain_k[...] = small[9:10, : gain_k.shape[1]]
     for source, target in zip(refs[:count], out):
         target[...] = source[...].astype(target.dtype)
     total = t_dot(hid_all[0, 0], ct_all[0])
@@ -1166,7 +1173,7 @@
     gd[...] = total
 
 
-def widen(arrays, kinds, hid_all, ct_all, shape):
+def widen(arrays, kinds, hid_all, ct_all, small, shape, size):
     members, rows_of, tokens, fw = hid_all.shape
     parts = 2 if fw % (2 * lanes) == 0 else 1
     steps = rows_of * parts
@@ -1175,7 +1182,12 @@
         return pl.BlockSpec((array_shape[0] // steps, array_shape[1]), lambda i: (i, 0))
 
     specs = [rows(array.shape) for array in arrays]
-    shapes = [array.shape for array in arrays] + [shape]
+    vectors = [(1, small.shape[1])] * 2 + [(1, size)] * 2
+    shapes = [array.shape for array in arrays] + [shape] + vectors
+
+    def whole(array_shape):
+        return pl.BlockSpec(array_shape, lambda i: (0,) * len(array_shape))
+
     return pl.pallas_call(
         widen_kernel,
         grid=(steps,),
@@ -1185,11 +1197,12 @@
             pl.BlockSpec(
                 (members, 1, tokens, fw // parts), lambda i: (0, i // parts, 0, i % parts)
             ),
-            pl.BlockSpec(ct_all.shape, lambda i: (0, 0, 0)),
+            whole(ct_all.shape),
+            whole(small.shape),
         ],
-        out_specs=tuple(specs + [rows(shape)]),
+        out_specs=tuple(specs + [rows(shape)] + [whole(vector) for vector in vectors]),
         compiler_params=pltpu.CompilerParams(vmem_limit_bytes=full_vmem),
-    )(*arrays, hid_all, ct_all)
+    )(*arrays, hid_all, ct_all, small)
 
 
 def vmem(shape, kind):
@@ -1263,10 +1276,9 @@
     heads = qw // size
     others, beside = max(rows_of - 1, 1), max(cols_of - 1, 1)
     half = size // 2
-    inverse = rope_base ** (-2.0 * jnp.arange(half, dtype=wide) / size)
-    inverse = jnp.concatenate([inverse, inverse])[None, :]
+    inverse = rope_base ** (-2.0 * np.arange(half) / size)
+    inverse = jnp.asarray(np.concatenate([inverse, inverse])[None, :], wide)
     seg_row = segments.reshape(1, tokens)
-    seg_col = segments.reshape(tokens, 1)
     gain1, gain2 = attention_norm[None, :], feedforward_norm[None, :]
     qn, kn = query_norm[None, :], key_norm[None, :]
     total = qw + 2 * kw
@@ -1297,15 +1309,20 @@
             ((tokens, lanes), wide),
             ((tokens, depth), low),
             ((tokens, fw), low),
-            ((tokens, 2 * fw), wide),
+            ((tokens, 2 * fw), low),
             ((members, tokens, depth), low),
         ),
         [
+            vmem((tokens, lanes), wide),
             vmem((tokens, depth), low),
             vmem((tokens, total), wide),
             vmem((others, tokens, total), low),
             vmem((others, tokens, total), low),
             vmem((2, tokens // 2, total), low),
+            vmem((tokens, fw), wide),
+            vmem((others, tokens, fw), low),
+            vmem((others, tokens, fw), low),
+            vmem((2, tokens // 2, fw), low),
             vmem((tokens, 2 * fw), wide),
             vmem((others, tokens, 2 * fw), low),
             vmem((others, tokens, 2 * fw), low),
@@ -1318,12 +1335,11 @@
         ]
         + sems(1)
         + [dma((peers,)), dma((peers,)), dma((1,))]
-        + [dma((2, max(6, others)))] * 2,
+        + [dma((3, max(6, others)))] * 2,
         0,
         dict(
             x=block_input,
             seg_row=seg_row,
-            seg_col=seg_col,
             inverse=inverse,
             gain1=gain1,
             wq=query_weight,
@@ -1336,13 +1352,14 @@
             wg=gate_weight,
             wu=up_weight,
             ct=cotangent,
+            wd=down_weight,
         ),
-        late=("wo", "wg", "wu", "ct"),
+        late=("wo", "wg", "wu", "ct", "wd"),
         outside=(12,),
     )
     *saved, ct_all = saved
     saved = dict(
-        zip(("n1", "fs", "raw", "lows", "shares", "trig", "mixed", "mid", "ss", "n2", "hid", "slope"), saved)
+        zip(("n1", "fs", "raw", "lows", "shares", "trig", "mixed", "mid", "ss", "n2", "hid", "gub"), saved)
     )
     weights = (query_weight, key_weight, value_weight, output_weight, gate_weight, up_weight)
     shapes = [weight.shape for weight in weights]
@@ -1365,9 +1382,6 @@
         ),
         [vmem(shape, low) for shape in shapes]
         + [
-            vmem((tokens, 2 * fw), low),
-            vmem((others, tokens, fw), low),
-            vmem((others, tokens, fw), low),
             vmem((others, tokens, fw), low),
             vmem((others, tokens, 2 * fw), low),
             vmem((depth, tokens), low),
@@ -1411,28 +1425,31 @@
             wu=up_weight,
             wd=down_weight,
         ),
-        late=("x", "n1", "fs", "raw", "lows", "shares", "trig", "mixed", "slope", "wq", "wk", "wv", "wo", "wg", "wu"),
+        late=("x", "n1", "fs", "raw", "lows", "shares", "trig", "mixed", "mid", "ss", "ct", "wd", "wq", "wk", "wv", "wo", "wg", "wu"),
         outside=range(3, 16),
     )
     block_output, input_gradient, small, hid_all, *partials = done[:10]
-    block_output, input_gradient, gq, gk, gv, go, gg, gu, gd = widen(
+    block_output, input_gradient, gq, gk, gv, go, gg, gu, gd, *sums = widen(
         (block_output, input_gradient, *partials),
-        [low] + [wide] * 8,
+        [low] + [wide] * 12,
         hid_all,
         ct_all,
+        small,
         down_weight.shape,
+        size,
     )
+    sum1, sum2, sum_q, sum_k = (vector[0] for vector in sums)
     return (
         block_output,
         input_gradient,
-        small[0],
+        sum1,
         gq,
         gk,
         gv,
-        small[8, :size],
-        small[9, :size],
+        sum_q,
+        sum_k,
         go,
-        small[1],
+        sum2,
         gg,
         gu,
         gd,

time: 415 us -> 397 us (0.957)
  Pallas kernels: 407 us -> 395 us
    pallas_call x2, Pallas kernels: 386 us -> 373 us  [call(): pl.pallas_call(body, out_shape=tuple((jax.ShapeDtypeStruct(shape, kind) f...]
where the time goes in v6:
time: 397 us; the launch traced here: 396 us
  Pallas kernels  395 us (99%)
    pallas_call x2, Pallas kernels, call(): pl.pallas_call(body, out_shape=tuple((jax.ShapeDtypeStruct(shape, kind) f...  373 us
    pallas_call x1, Pallas kernels, widen(): pl.pallas_call(widen_kernel, grid=(steps,), out_shape=tuple(map(jax.Shape...  21.3 us

profile of v6, /device:TPU:0, one launch (start us, length us, event | category | flops | bytes accessed | tf_op | source)
XLA Modules:
  0.0 395.5 jit_solution(13445516300180925803)
XLA Ops:
  0.6 109.6 %shard_map.246 = (bf16[384,512]{1,0:T(8,128)(2,1)}, f32[384,128]{1,0:T(8,128)}, f32[384,384]{1,0:T(8,128)}, bf16[384,512]{1,0:T(8,128)(2,1)}, f32[2,384,384]{2,1...) custom-call(bf16[384,512]{1,0:T(8,128)(2,1)} %refs_0_.3, ...), custom_call_target="tpu_custom_call" | custom-call | tf_op jit(solution)/shard_map/pallas_call | solution.py:1242
  110.2 263.9 %shard_map.247 = (bf16[384,512]{1,0:T(8,128)(2,1)}, f32[384,512]{1,0:T(8,128)}, f32[16,512]{1,0:T(8,128)}, bf16[4,4,384,768]{3,2,1,0:T(8,128)(2,1)}, bf16[512,10...) custom-call(bf16[384,512]{1,0:T(8,128)(2,1)} %refs_0_.3, ...), custom_call_target="tpu_custom_call" | custom-call | tf_op jit(solution)/shard_map/pallas_call | solution.py:1242
  374.1 21.3 %shard_map.248 = (bf16[384,512]{1,0:T(8,128)(2,1)}, f32[384,512]{1,0:T(8,128)}, f32[512,1024]{1,0:T(8,128)}, f32[512,512]{1,0:T(8,128)}, f32[512,512]{1,0:T(8,12...) custom-call(bf16[384,512]{1,0:T(8,128)(2,1)} %get-tuple-element.61.r, ...), custom_call_target="tpu_custom_call" | custom-call | tf_op jit(solution)/shard_map/pallas_call | solution.py:1191
